TPU v7x, 32 devices: a whole 2x2x4 slice. The times are simulated.
32 devices in a mesh: dp: 16 (over z, x, core), head: 2 (over y).
Axes of the slice: x: 2, y: 2, z: 4, core: 2. Of those that a mesh axis runs over, the one named last changes fastest.
Arguments:
- frames_in: bfloat16 [16, 2, 320, 2560], P('dp', 'head'), may hold values from -6 to 6
- ln1_gain: float32 [1280], replicated, may hold values from 0.25 to 1.75
- ln1_bias: float32 [1280], replicated, may hold values from -3 to 3
- qkv_weight: bfloat16 [1280, 3, 1024], P('dp', None, 'head'), may hold values from -0.1875 to 0.1875
- qv_bias: float32 [2, 1024], P(None, 'head'), may hold values from -3 to 3
- out_weight: bfloat16 [1024, 1280], P(('head', 'dp')), may hold values from -0.1875 to 0.1875
- out_bias: float32 [1280], P('head'), may hold values from -3 to 3
- ln2_gain: float32 [1280], replicated, may hold values from 0.25 to 1.75
- ln2_bias: float32 [1280], replicated, may hold values from -3 to 3
- fc1_weight: bfloat16 [1280, 5120], P('dp', 'head'), may hold values from -0.15625 to 0.15625
- fc1_bias: float32 [5120], P('head'), may hold values from -3 to 3
- fc2_weight: bfloat16 [5120, 1280], P(('head', 'dp')), may hold values from -0.078125 to 0.078125
- fc2_bias: float32 [1280], P('head'), may hold values from -3 to 3
- server_of_clip: int32 [16], replicated, may hold values from 0 to 7
Outputs:
- encoded: bfloat16 [16, 2, 320, 2560], P('dp', 'head')
All inputs are finite; a program needn't handle non-finite values.
Results may differ from a plain program's by a relative error of at most 0.014.
Values may be sent and summed in bfloat16 or wider, within the bound.
A program may use at most 64 MiB of HBM per device.

v0:
```python
import functools

import jax
import jax.numpy as jnp
from jax import lax
from jax.experimental import pallas as pl
from jax.experimental.pallas import tpu as pltpu
from jax.sharding import PartitionSpec as P

HDIM = 64


epsilon = 1e-05


def layer_norm(matrix, gain_row, shift_row):
    floats = matrix.astype(jnp.float32)
    center = jnp.mean(floats, axis=-1, keepdims=True)
    spread = jnp.mean(jnp.square(floats - center), axis=-1, keepdims=True)
    return ((floats - center) * lax.rsqrt(spread + epsilon) * gain_row + shift_row).astype(
        jnp.bfloat16
    )


def normalize(residual_in, gain_row, shift_row):
    whole_rows = lax.all_gather(residual_in, "head", axis=1, tiled=True)
    return layer_norm(whole_rows, gain_row, shift_row)


def attend(queries, key_rows, value_rows):

    def single(triple):
        query_head, key_head, value_head = triple
        scores = jnp.dot(query_head, key_head.T, preferred_element_type=jnp.float32)
        maxima = jnp.max(scores, axis=-1, keepdims=True)
        weights = jnp.exp(scores - maxima)
        probability = (weights / jnp.sum(weights, axis=-1, keepdims=True)).astype(jnp.bfloat16)
        return jnp.dot(probability, value_head, preferred_element_type=jnp.float32).astype(
            jnp.bfloat16
        )

    per_head = lax.map(
        single,
        (jnp.swapaxes(queries, 0, 1), jnp.swapaxes(key_rows, 0, 1), jnp.swapaxes(value_rows, 0, 1)),
    )
    return jnp.swapaxes(per_head, 0, 1).reshape(queries.shape[0], -1)


def slot_order(server_list):
    clip_count = server_list.shape[0]
    indices = jnp.arange(clip_count, dtype=jnp.int32)
    earlier = (server_list[None, :] < server_list[:, None]) | (
        server_list[None, :] == server_list[:, None]
    ) & (indices[None, :] < indices[:, None])
    slot_of = jnp.sum(earlier.astype(jnp.int32), axis=1)
    return jnp.sum(jnp.where(slot_of[None, :] == indices[:, None], indices[None, :], 0), axis=1)


def regroup(block_rows, clip_order):
    group_size = lax.axis_size("dp")
    piece_rows = block_rows.reshape(group_size, -1)
    shuffled = lax.all_to_all(piece_rows, "dp", split_axis=0, concat_axis=0, tiled=True)
    picked = jnp.take(shuffled, clip_order, axis=0)
    returned = lax.all_to_all(picked, "dp", split_axis=0, concat_axis=0, tiled=True)
    return returned.reshape(block_rows.shape)


def block_term(operand, weight_rows, row_count, frame_count, local_width):
    blocks = row_count // frame_count
    product = jnp.dot(operand, weight_rows, preferred_element_type=jnp.float32)
    return (
        product.reshape(frame_count, blocks, local_width)
        .transpose(1, 0, 2)
        .reshape(blocks * frame_count, local_width)
    )


def on_device(
    frames_in,
    ln1_gain,
    ln1_bias,
    qkv_weight,
    qv_bias,
    out_weight,
    out_bias,
    ln2_gain,
    ln2_bias,
    fc1_weight,
    fc1_bias,
    fc2_weight,
    fc2_bias,
    server_of_clip,
):
    clip_order = slot_order(server_of_clip)
    group_rows = frames_in.shape[2]
    local_width = frames_in.shape[3] // 4
    frame_count = group_rows * 4
    residual_in = frames_in[0, 0].reshape(frame_count, local_width)
    residual_in = regroup(residual_in, clip_order)
    normed_one = normalize(residual_in, ln1_gain, ln1_bias)
    column_count = qkv_weight.shape[2]
    weight_piece = lax.all_gather(qkv_weight, "dp", axis=0, tiled=True)
    operand = normed_one
    projected = jnp.dot(
        operand, weight_piece.reshape(weight_piece.shape[0], -1), preferred_element_type=jnp.float32
    ).reshape(frame_count, 3, column_count)
    queries = (
        ((projected[:, 0] + qv_bias[0]) * HDIM ** (-0.5))
        .astype(jnp.bfloat16)
        .reshape(frame_count, -1, HDIM)
    )
    key_rows = projected[:, 1].astype(jnp.bfloat16).reshape(frame_count, -1, HDIM)
    value_rows = (projected[:, 2] + qv_bias[1]).astype(jnp.bfloat16).reshape(frame_count, -1, HDIM)
    context = attend(queries, key_rows, value_rows)
    output_rows = lax.all_gather(out_weight, "dp", axis=0, tiled=True)
    carried = residual_in.astype(jnp.float32) + out_bias
    attended = (
        carried
        + lax.psum_scatter(
            block_term(
                context, output_rows, frame_count * lax.axis_size("head"), frame_count, local_width
            ).astype(jnp.bfloat16),
            "head",
            scatter_dimension=0,
            tiled=True,
        ).astype(jnp.float32)
    ).astype(jnp.bfloat16)
    normed_two = normalize(attended, ln2_gain, ln2_bias)
    operand = normed_two
    hidden_sums = jnp.dot(
        operand,
        lax.all_gather(fc1_weight, "dp", axis=0, tiled=True),
        preferred_element_type=jnp.float32,
    )
    hidden = jax.nn.gelu(hidden_sums + fc1_bias, approximate=False).astype(jnp.bfloat16)
    down_rows = lax.all_gather(fc2_weight, "dp", axis=0, tiled=True)
    kept = attended.astype(jnp.float32) + fc2_bias
    layer_out = (
        kept
        + lax.psum_scatter(
            block_term(
                hidden, down_rows, frame_count * lax.axis_size("head"), frame_count, local_width
            ).astype(jnp.bfloat16),
            "head",
            scatter_dimension=0,
            tiled=True,
        ).astype(jnp.float32)
    ).astype(jnp.bfloat16)
    return layer_out.reshape(1, 1, group_rows, 4 * local_width)


MESH = pl.DeviceIdType.MESH
VMEM = pltpu.MemorySpace.VMEM
LIMIT = 60000000


def at_rows(index, rows):
    return pl.ds(pl.multiple_of(index * rows, rows), rows)


def greet(peers):
    barrier = pltpu.get_barrier_semaphore()
    for peer in peers:
        pl.semaphore_signal(barrier, inc=1, device_id=peer, device_id_type=MESH)
    pl.semaphore_wait(barrier, len(peers))


def regroup_kernel(dp, heads, order_ref, x_ref, o_ref, first, second, s1, r1, s2, r2, s3, r3):
    me, h = lax.axis_index("dp"), lax.axis_index("head")
    rows, width = first.shape[1:]
    row_blocks = x_ref.shape[0] // rows
    greet(
        [(lax.rem(me + k, dp), h) for k in range(1, dp)]
        + [(me, lax.rem(h + j, heads)) for j in range(1, heads)]
    )

    def taken(c):
        return x_ref.at[
            at_rows(lax.rem(c, row_blocks), rows), at_rows(lax.div(c, row_blocks), width)
        ]

    def placed(c):
        return o_ref.at[at_rows(c, rows), at_rows(h, width)]

    def one(k):
        other = lax.rem(me + k, dp)
        return pltpu.make_async_remote_copy(
            taken(other), first.at[me], s1.at[k], r1.at[k], (other, h), MESH
        )

    def two(k):
        other = lax.rem(me + k, dp)
        return pltpu.make_async_remote_copy(
            second.at[other], placed(me), s2.at[k], r2.at[k], (other, h), MESH
        )

    def three(k, j):
        ref = placed(lax.rem(me - k + dp, dp))
        return pltpu.make_async_remote_copy(
            ref, ref, s3.at[j - 1, k], r3.at[j - 1, k], (me, lax.rem(h + j, heads)), MESH
        )

    def loop(start, body):
        def step(k, carry):
            body(k)
            return carry

        lax.fori_loop(start, dp, step, 0)

    loop(1, lambda k: one(k).start())
    own = pltpu.make_async_copy(taken(me), first.at[me], r1.at[0])
    own.start()
    own.wait()
    loop(1, lambda k: one(k).wait_recv())

    def pick(k):
        other = lax.rem(me + k, dp)
        second[other] = first[order_ref[other]]

    loop(0, pick)
    loop(1, lambda k: two(k).start())
    own = pltpu.make_async_copy(second.at[me], placed(me), r2.at[0])
    own.start()
    own.wait()
    for j in range(1, heads):
        three(0, j).start()

    def forward(k):
        two(k).wait_recv()
        for j in range(1, heads):
            three(k, j).start()

    loop(1, forward)

    def finish(k):
        for j in range(1, heads):
            three(k, j).wait()

    loop(0, finish)
    loop(1, lambda k: one(k).wait_send())
    loop(1, lambda k: two(k).wait_send())


def regroup_gather(frames, clip_order, dp, heads, width):
    groups = frames.shape[0]
    rows = groups * 4 // dp
    sems = [pltpu.SemaphoreType.DMA((dp,))] * 4 + [pltpu.SemaphoreType.DMA((heads - 1, dp))] * 2
    return pl.pallas_call(
        functools.partial(regroup_kernel, dp, heads),
        out_shape=jax.ShapeDtypeStruct((groups * 4, heads * width), frames.dtype),
        in_specs=[
            pl.BlockSpec(memory_space=pltpu.MemorySpace.SMEM),
            pl.BlockSpec(memory_space=VMEM),
        ],
        out_specs=pl.BlockSpec(memory_space=VMEM),
        scratch_shapes=[pltpu.VMEM((dp, rows, width), frames.dtype)] * 2 + sems,
        compiler_params=pltpu.CompilerParams(
            collective_id=0, has_side_effects=True, vmem_limit_bytes=24000000
        ),
        cost_estimate=pl.CostEstimate(flops=0, bytes_accessed=200000000, transcendentals=0),
        name="regroup",
    )(clip_order, frames)


def norm_rows(floats, gain, shift):
    center = jnp.mean(floats, axis=-1, keepdims=True)
    moved = floats - center
    spread = jnp.mean(jnp.square(moved), axis=-1, keepdims=True)
    return (moved * lax.rsqrt(spread + epsilon) * gain + shift).astype(jnp.bfloat16)


def project_kernel(x_ref, gain_ref, shift_ref, w_ref, b_ref, q_ref, k_ref, v_ref):
    n = q_ref.shape[1]
    normed = norm_rows(x_ref[...].astype(jnp.float32), gain_ref[...], shift_ref[...])

    def part(i):
        return jnp.dot(normed, w_ref[:, i * n : (i + 1) * n], preferred_element_type=jnp.float32)

    q_ref[...] = ((part(0) + b_ref[0:1]) * HDIM ** (-0.5)).astype(jnp.bfloat16)
    k_ref[...] = part(1).astype(jnp.bfloat16)
    v_ref[...] = (part(2) + b_ref[1:2]).astype(jnp.bfloat16)


def project(x, gain, shift, weight, bias, block):
    rows, depth = x.shape
    n = weight.shape[1] // 3
    whole = pl.BlockSpec(memory_space=VMEM)
    spec = pl.BlockSpec((block, n), lambda i: (i, 0))
    return pl.pallas_call(
        project_kernel,
        grid=(rows // block,),
        out_shape=[jax.ShapeDtypeStruct((rows, n), jnp.bfloat16)] * 3,
        in_specs=[pl.BlockSpec((block, depth), lambda i: (i, 0)), whole, whole, whole, whole],
        out_specs=[spec] * 3,
        compiler_params=pltpu.CompilerParams(vmem_limit_bytes=32000000),
        cost_estimate=pl.CostEstimate(
            flops=2 * rows * depth * 3 * n, bytes_accessed=12000000, transcendentals=0
        ),
        name="project",
    )(x, gain, shift, weight, bias)


def attend_kernel(
    dp, heads, block, q_ref, k_ref, v_ref, w_ref, o_ref, all_ref, send, recv, ys, yr, ws, wr, own_sem
):
    me, h = lax.axis_index("dp"), lax.axis_index("head")
    frames, columns = q_ref.shape
    pair = 2 * HDIM
    pairs = columns // pair
    greet(
        [(me, lax.rem(h + j, heads)) for j in range(1, heads)]
        + [(lax.rem(me + k, dp), h) for k in range(1, dp)]
    )

    def weight_rows(j):
        index = lax.rem(h + j, heads) * dp + me
        return all_ref.at[at_rows(index, w_ref.shape[0])]

    def across(j):
        return pltpu.make_async_remote_copy(
            w_ref, weight_rows(0), ys.at[j - 1], yr.at[j - 1], (me, lax.rem(h + j, heads)), MESH
        )

    def along(k, j):
        ref = weight_rows(j)
        return pltpu.make_async_remote_copy(
            ref, ref, ws.at[j, k], wr.at[j, k], (lax.rem(me + k, dp), h), MESH
        )

    for j in range(1, heads):
        across(j).start()
    mine = pltpu.make_async_copy(w_ref, weight_rows(0), own_sem)
    mine.start()
    mine.wait()

    def start_along(j):
        def step(k, carry):
            along(k, j).start()
            return carry

        lax.fori_loop(1, dp, step, 0)

    start_along(0)
    for j in range(1, heads):
        across(j).wait()
    for j in range(1, heads):
        start_along(j)
    lane = lax.broadcasted_iota(jnp.int32, (1, pair), 1)
    low_f = jnp.where(lane < HDIM, 1.0, 0.0)
    low, high = low_f.astype(jnp.bfloat16), (1.0 - low_f).astype(jnp.bfloat16)

    def copy(p, j):
        ref = o_ref.at[:, at_rows(h * pairs + p, pair)]
        return pltpu.make_async_remote_copy(
            ref, ref, send.at[j - 1, p], recv.at[j - 1, p], (me, lax.rem(h + j, heads)), MESH
        )

    def each_pair(p, carry):
        cols = at_rows(p, pair)
        keys, values = k_ref[:, cols], v_ref[:, cols]
        value_low, value_high = values * low + high, values * high + low

        def head(query, value):
            scores = lax.dot_general(
                query, keys, (((1,), (1,)), ((), ())), preferred_element_type=jnp.float32
            )
            top = jnp.max(scores, axis=-1, keepdims=True)
            weights = jnp.exp(scores - top).astype(jnp.bfloat16)
            return jnp.dot(weights, value, preferred_element_type=jnp.float32)

        def each_block(b, inner):
            rows = at_rows(b, block)
            query = q_ref[rows, cols]
            first = head(query * low, value_low)
            second = head(query * high, value_high)
            top = first * low_f + second * (1.0 - low_f)
            total = pltpu.roll(first * (1.0 - low_f) + second * low_f, HDIM, 1)
            o_ref[rows, at_rows(h * pairs + p, pair)] = (top / total).astype(jnp.bfloat16)
            return inner

        lax.fori_loop(0, frames // block, each_block, 0)
        for j in range(1, heads):
            copy(p, j).start()
        return carry

    lax.fori_loop(0, pairs, each_pair, 0)

    def finish(p, carry):
        for j in range(1, heads):
            copy(p, j).wait()
        return carry

    lax.fori_loop(0, pairs, finish, 0)

    def finish_along(k, carry):
        for j in range(heads):
            along(k, j).wait()
        return carry

    lax.fori_loop(1, dp, finish_along, 0)


def attend_gather(q, k, v, weight, dp, heads, block):
    frames, columns = q.shape
    pairs = columns // (2 * HDIM)
    whole = pl.BlockSpec(memory_space=VMEM)
    return pl.pallas_call(
        functools.partial(attend_kernel, dp, heads, block),
        out_shape=[
            jax.ShapeDtypeStruct((frames, heads * columns), q.dtype),
            jax.ShapeDtypeStruct((heads * dp * weight.shape[0], weight.shape[1]), weight.dtype),
        ],
        in_specs=[whole] * 4,
        out_specs=[whole] * 2,
        scratch_shapes=[pltpu.SemaphoreType.DMA((heads - 1, pairs))] * 2
        + [pltpu.SemaphoreType.DMA((heads - 1,))] * 2
        + [pltpu.SemaphoreType.DMA((heads, dp))] * 2
        + [pltpu.SemaphoreType.DMA],
        compiler_params=pltpu.CompilerParams(
            collective_id=1, has_side_effects=True, vmem_limit_bytes=32000000
        ),
        cost_estimate=pl.CostEstimate(
            flops=20000000000, bytes_accessed=6000000, transcendentals=13000000
        ),
        name="attend",
    )(q, k, v, weight)


def output_kernel(x_ref, c_ref, w_ref, bias_ref, gain_ref, shift_ref, a_ref, n_ref):
    product = jnp.dot(c_ref[...], w_ref[...], preferred_element_type=jnp.float32)
    attended = (x_ref[...].astype(jnp.float32) + bias_ref[...] + product).astype(jnp.bfloat16)
    a_ref[...] = attended
    n_ref[...] = norm_rows(attended.astype(jnp.float32), gain_ref[...], shift_ref[...])


def output_norm(x, context, weight, bias, gain, shift, block):
    rows, depth = x.shape
    whole = pl.BlockSpec(memory_space=VMEM)
    spec = pl.BlockSpec((block, depth), lambda i: (i, 0))
    return pl.pallas_call(
        output_kernel,
        grid=(rows // block,),
        out_shape=[jax.ShapeDtypeStruct((rows, depth), jnp.bfloat16)] * 2,
        in_specs=[
            spec,
            pl.BlockSpec((block, context.shape[1]), lambda i: (i, 0)),
            whole,
            whole,
            whole,
            whole,
        ],
        out_specs=[spec] * 2,
        compiler_params=pltpu.CompilerParams(vmem_limit_bytes=32000000),
        cost_estimate=pl.CostEstimate(
            flops=2 * rows * depth * context.shape[1], bytes_accessed=14000000, transcendentals=0
        ),
        name="output",
    )(x, context, weight, bias, gain, shift)


def feed_kernel(
    heads, tile, n_ref, a_ref, w1_ref, b1_ref, w2_ref, b2_ref, o_ref, hidden, kept, out, got, s, r
):
    me, h = lax.axis_index("dp"), lax.axis_index("head")
    blocks, rows, width = kept.shape
    greet([(me, lax.rem(h + j, heads)) for j in range(1, heads)])

    def copy(b, j):
        return pltpu.make_async_remote_copy(
            out.at[j - 1, b],
            got.at[j - 1, b],
            s.at[j - 1, b],
            r.at[j - 1, b],
            (me, lax.rem(h + j, heads)),
            MESH,
        )

    def share(target):
        return jnp.dot(
            hidden[...], w2_ref[:, at_rows(target, width)], preferred_element_type=jnp.float32
        )

    def each_block(b, carry):
        at = at_rows(b, rows)

        def each_tile(t, inner):
            cols = at_rows(t, tile)
            sums = jnp.dot(n_ref[at, :], w1_ref[:, cols], preferred_element_type=jnp.float32)
            sums = sums + b1_ref[:, cols]
            hidden[:, cols] = (0.5 * sums * (1.0 + lax.erf(sums * 0.7071067811865476))).astype(
                jnp.bfloat16
            )
            return inner

        lax.fori_loop(0, w1_ref.shape[1] // tile, each_tile, 0)
        for j in range(1, heads):
            out[j - 1, b] = share(lax.rem(h + j, heads)).astype(jnp.bfloat16)
            copy(b, j).start()
        kept[b] = a_ref[at, at_rows(h, width)].astype(jnp.float32) + b2_ref[...] + share(h)
        return carry

    lax.fori_loop(0, blocks, each_block, 0)
    for b in range(blocks):
        total = kept[b]
        for j in range(1, heads):
            copy(b, j).wait()
            total = total + got[j - 1, b].astype(jnp.float32)
        o_ref[:, b * width : (b + 1) * width] = total.astype(jnp.bfloat16)


def feed_forward(normed, attended, w1, b1, w2, b2, heads, tile):
    frames, depth = normed.shape
    width = depth // heads
    rows = frames // 4
    whole = pl.BlockSpec(memory_space=VMEM)
    return pl.pallas_call(
        functools.partial(feed_kernel, heads, tile),
        out_shape=jax.ShapeDtypeStruct((rows, 4 * width), jnp.bfloat16),
        in_specs=[whole] * 6,
        out_specs=whole,
        scratch_shapes=[
            pltpu.VMEM((rows, w1.shape[1]), jnp.bfloat16),
            pltpu.VMEM((4, rows, width), jnp.float32),
            pltpu.VMEM((heads - 1, 4, rows, width), jnp.bfloat16),
            pltpu.VMEM((heads - 1, 4, rows, width), jnp.bfloat16),
            pltpu.SemaphoreType.DMA((heads - 1, 4)),
            pltpu.SemaphoreType.DMA((heads - 1, 4)),
        ],
        compiler_params=pltpu.CompilerParams(
            collective_id=2, has_side_effects=True, vmem_limit_bytes=LIMIT
        ),
        cost_estimate=pl.CostEstimate(
            flops=4 * frames * depth * w1.shape[1], bytes_accessed=40000000, transcendentals=0
        ),
        name="feed",
    )(normed, attended, w1, b1, w2, b2)


def on_device_aligned(
    frames_in,
    ln1_gain,
    ln1_bias,
    qkv_weight,
    qv_bias,
    out_weight,
    out_bias,
    ln2_gain,
    ln2_bias,
    fc1_weight,
    fc1_bias,
    fc2_weight,
    fc2_bias,
    server_of_clip,
):
    dp, heads = lax.axis_size("dp"), lax.axis_size("head")
    width = frames_in.shape[3] // 4
    block = frames_in.shape[2] * 4 // 5
    whole_bias = lax.all_gather(out_bias, "head", axis=0, tiled=True)
    w_qkv = lax.all_gather(
        qkv_weight.reshape(qkv_weight.shape[0], -1), "dp", axis=0, tiled=True
    )
    w_up = lax.all_gather(fc1_weight, "dp", axis=0, tiled=True)
    w_down = lax.all_gather(fc2_weight, "dp", axis=0, tiled=True)
    residual = regroup_gather(frames_in[0, 0], slot_order(server_of_clip), dp, heads, width)
    q, k, v = project(residual, ln1_gain[None], ln1_bias[None], w_qkv, qv_bias, block)
    context, w_out = attend_gather(q, k, v, out_weight, dp, heads, block)
    attended, normed = output_norm(
        residual, context, w_out, whole_bias[None], ln2_gain[None], ln2_bias[None], block
    )
    layer_out = feed_forward(
        normed, attended, w_up, fc1_bias[None], w_down, fc2_bias[None], heads, block * 2
    )
    return layer_out[None, None]


def aligned(mesh, frames_in, qkv_weight, out_weight, fc1_weight):
    dp, heads = mesh.shape["dp"], mesh.shape["head"]
    groups, width = frames_in.shape[2], frames_in.shape[3] // 4
    frames = groups * 4
    return (
        dp % 4 == 0
        and heads > 1
        and frames % dp == 0
        and groups % (frames // dp) == 0
        and (frames // dp) % 16 == 0
        and frames % 80 == 0
        and width % 128 == 0
        and out_weight.shape[0] % (dp * heads * 16) == 0
        and (qkv_weight.shape[2] // heads) % (2 * HDIM) == 0
        and (fc1_weight.shape[1] // heads) % (frames // 5 * 2) == 0
    )


def solution(mesh):
    placed = (
        P("dp", "head", None, None),
        P(),
        P(),
        P("dp", None, "head"),
        P(None, "head"),
        P(("head", "dp"), None),
        P("head"),
        P(),
        P(),
        P("dp", "head"),
        P("head"),
        P(("head", "dp"), None),
        P("head"),
        P(),
    )

    def layer(*args):
        body = on_device_aligned if aligned(mesh, args[0], args[3], args[5], args[9]) else on_device
        return jax.shard_map(
            body,
            mesh=mesh,
            in_specs=placed,
            out_specs=P("dp", "head", None, None),
            check_vma=False,
        )(*args)

    return layer
```

profile of v0, /device:TPU:27, one launch (start us, length us, event | category | flops | bytes accessed | tf_op | source)
XLA Modules:
  0.0 325.6 jit_solution(10368391156039031710)
XLA Ops:
  6.5 0.0 all-gather.5.cloned.1.call-start
  6.5 1.7 copy.19
  8.2 0.0 all-gather.5.cloned.1.call-update
  8.2 0.0 all-gather.7.cloned.1.call-start
  8.3 0.7 all-gather.7.cloned.1.call-update
  9.0 0.0 copy-start.3
  9.0 0.0 all-gather.9.cloned.1.call-start
  9.0 0.7 all-gather.9.cloned.1.call-update
  9.7 0.7 broadcast_in_dim.44.gain_ref
  10.4 0.7 broadcast_in_dim.45.shift_ref
  11.1 0.7 reshape.7
  11.8 0.7 broadcast_in_dim.47.gain_ref
  12.5 0.7 broadcast_in_dim.48.shift_ref
  13.2 1.3 broadcast_in_dim.49.b1_ref
  14.5 1.3 broadcast_in_dim.50.b2_ref
  15.8 0.9 convert_reduce_fusion
  16.7 0.1 select_reduce_fusion.order_ref
  16.8 1.4 copy-done
  18.3 123.1 %regroup.1.x_ref = bf16[1280,1280]{1,0:T(8,128)(2,1)S(1)} custom-call(s32[16]{0:T(128)S(1)} %select_reduce_fusion.order_ref, bf16[320,2560]{1,0:T(8,128)(2,1)S(1)} %bitcast.5), custom_call_target="tpu_custom_call" | custom-call | bytes 200000000 | tf_op jit(solution)/shard_map/regroup/pallas_call | solution.py:248
  141.4 3.5 %all-gather = f32[2,1,640]{2,1,0:T(1,128)S(1)} all-gather(f32[1,1,640]{2,1,0:T(1,128)S(1)} %reshape.7), channel_id=1, replica_groups=mesh['dp'=16,'head'=2] {'head'}, dimensions={0}, use_global_device_ids=true | all-gather | bytes 7680 | tf_op jit(solution)/shard_map/all_gather | solution.py:558
  144.9 0.0 copy-done.3
  144.9 2.1 copy-done.1
  147.0 7.8 %project.1 = (bf16[1280,512]{1,0:T(8,128)(2,1)S(1)}, bf16[1280,512]{1,0:T(8,128)(2,1)S(1)}, bf16[1280,512]{1,0:T(8,128)(2,1)S(1)}) custom-call(bf16[1280,1280]{1,0:T(8,128)(2,1)S(1)} %regroup.1.x_ref, f32[1,1280]{1,0:T(1,128)S(1)} %broadcast_in_dim.44.gain_ref, f32[1,1280]{1,0:T(1,128)S(1)} %broadcast_in_dim.45.shift_ref, bf16[1280,1536]{1,0:T(8,128)(2,1)S(1)} %copy-done.1, ...), custom_call_target="tpu_custom_call" | custom-call | flops 5033164800 | bytes 12000000 | tf_op jit(solution)/shard_map/project/pallas_call | solution.py:289
  154.9 0.0 copy-done.2
  154.9 83.0 %attend.1 = (bf16[1280,1024]{1,0:T(8,128)(2,1)S(1)}, bf16[1024,1280]{1,0:T(8,128)(2,1)S(1)}) custom-call(bf16[1280,512]{1,0:T(8,128)(2,1)S(1)} %get-tuple-element.12.q_ref, bf16[1280,512]{1,0:T(8,128)(2,1)S(1)} %get-tuple-element.13.k_ref, bf16[1280,512]{1,0:T(8,128)(2,1)S(1)} %get-tuple-element.14.v_ref, bf16[32,1280]{1,0:T(8,128)(2,1)S(1)} %copy-done.2), custom_call_target="tpu_custom_call" | custom-call | flops 20000000000 | bytes 6000000 | tf_op jit(solution)/shard_map/attend/pallas_call | solution.py:407
  237.9 6.3 %output.1 = (bf16[1280,1280]{1,0:T(8,128)(2,1)S(1)}, bf16[1280,1280]{1,0:T(8,128)(2,1)S(1)}) custom-call(bf16[1280,1280]{1,0:T(8,128)(2,1)S(1)} %regroup.1.x_ref, bf16[1280,1024]{1,0:T(8,128)(2,1)S(1)} %get-tuple-element.15.c_ref, bf16[1024,1280]{1,0:T(8,128)(2,1)S(1)} %get-tuple-element.16.w_ref, f32[1,1280]{1,0:T(1,128)S(1)} %bitcast.6, ...), custom_call_target="tpu_custom_call" | custom-call | flops 3355443200 | bytes 14000000 | tf_op jit(solution)/shard_map/output/pallas_call | solution.py:440
  244.2 0.0 copy-start.4
  244.2 1.7 copy-done.4
  245.9 1.7 copy-done.5
  247.6 18.5 %all-gather.9.cloned.1.call-done.w2_ref = bf16[2560,1280]{1,0:T(8,128)(2,1)} async-done(((bf16[160,1280]{1,0:T(8,128)(2,1)}), bf16[2560,1280]{1,0:T(8,128)(2,1)}) %all-gather.9.cloned.1.call-update) | async-done | bytes 6553616 | tf_op jit(solution)/shard_map/all_gather | solution.py:563
  266.1 50.2 %feed.1 = bf16[320,2560]{1,0:T(8,128)(2,1)} custom-call(bf16[1280,1280]{1,0:T(8,128)(2,1)} %copy-done.5, bf16[1280,1280]{1,0:T(8,128)(2,1)} %copy-done.4, bf16[1280,2560]{1,0:T(8,128)(2,1)} %all-gather.7.cloned.1.call-done.w1_ref, f32[1,2560]{1,0:T(1,128)} %broadcast_in_dim.49.b1_ref, bf16[2560,1280]{1,0:T(8,128)(2,1)} %all-gather.9.cloned.1.call-done.w2_ref, ...), custom_call_target="tpu_custom_call" | custom-call | flops 16777216000 | bytes 40000000 | tf_op jit(solution)/shard_map/feed/pallas_call | solution.py:516
  316.4 2.7 copy.21
  (6 shorter events, 0.0 us)
Async XLA Ops:
  6.5 138.4 %all-gather.5.cloned.1.call-start = ((), (), s32[]{:S(2)}) async-start(), calls=%async_computation | async-start | bytes 4177920 | tf_op jit(solution)/shard_map/all_gather | solution.py:559
  8.2 239.4 %all-gather.7.cloned.1.call-start = ((), (), s32[]{:S(2)}) async-start(), calls=%async_computation.1 | async-start | bytes 6963200 | tf_op jit(solution)/shard_map/all_gather | solution.py:562
  9.0 135.9 %copy-start.3 = (f32[2,512]{1,0:T(2,128)S(1)}, f32[2,512]{1,0:T(2,128)}, u32[]{:S(2)}) copy-start(f32[2,512]{1,0:T(2,128)} %b_ref.1) | copy-start | bytes 12292
  9.0 257.1 %all-gather.9.cloned.1.call-start = ((), (), s32[]{:S(2)}) async-start(), calls=%async_computation.2 | async-start | bytes 6963200 | tf_op jit(solution)/shard_map/all_gather | solution.py:563
  16.8 1.4 copy-start
  144.9 2.1 copy-start.1
  147.0 7.8 %copy-start.2 = (bf16[32,1280]{1,0:T(8,128)(2,1)S(1)}, bf16[32,1280]{1,0:T(8,128)(2,1)}, u32[]{:S(2)}) copy-start(bf16[32,1280]{1,0:T(8,128)(2,1)} %w_ref.1) | copy-start | bytes 245764
  244.2 1.7 copy-start.4
  245.9 1.7 copy-start.5
Sparse Core Ops, SparseCore 0:
  9.6 79.3 all-gather.4
  91.3 81.9 all-gather.6
  175.5 90.5 all-gather.8
where the time goes:
time: 330 us; the launch traced here: 326 us
  Pallas kernels  270 us (82%)
  waiting for transfers between devices  19.9 us (6%)
  local copies, waits for them, and re-layouts  17.3 us (5%)
  between operations  13.2 us (4%)
  blocking collectives  3.53 us (1%)
    pallas_call x1, Pallas kernels, regroup_gather(): pl.pallas_call(functools.partial(regroup_kernel, dp, heads), out_shape=ja...  123 us
    pallas_call x1, Pallas kernels, attend_gather(): pl.pallas_call(functools.partial(attend_kernel, dp, heads, block), out_sh...  83 us
    pallas_call x1, Pallas kernels, feed_forward(): pl.pallas_call(functools.partial(feed_kernel, heads, tile), out_shape=jax...  50.2 us
    all_gather x1, waiting for transfers between devices, on_device_aligned(): w_down = lax.all_gather(fc2_weight, 'dp', axis=0, tiled=True)  18.5 us
    unnamed x14, local copies, waits for them, and re-layouts  10.3 us
    pallas_call x1, Pallas kernels, project(): pl.pallas_call(project_kernel, grid=(rows // block,), out_shape=[jax.Shap...  7.84 us
  transfers between devices with their start and end apart: 3, of which 1 were waited for; matrix products, arithmetic and copies ran while one was open for 2% of the time, Pallas kernels for 68%

commit v1 on v0

v1 whole, which is shorter than its diff:
```python
import functools

import jax
import jax.numpy as jnp
from jax import lax
from jax.experimental import pallas as pl
from jax.experimental.pallas import tpu as pltpu
from jax.sharding import PartitionSpec as P

HDIM = 64


epsilon = 1e-05


def layer_norm(matrix, gain_row, shift_row):
    floats = matrix.astype(jnp.float32)
    center = jnp.mean(floats, axis=-1, keepdims=True)
    spread = jnp.mean(jnp.square(floats - center), axis=-1, keepdims=True)
    return ((floats - center) * lax.rsqrt(spread + epsilon) * gain_row + shift_row).astype(
        jnp.bfloat16
    )


def normalize(residual_in, gain_row, shift_row):
    whole_rows = lax.all_gather(residual_in, "head", axis=1, tiled=True)
    return layer_norm(whole_rows, gain_row, shift_row)


def attend(queries, key_rows, value_rows):

    def single(triple):
        query_head, key_head, value_head = triple
        scores = jnp.dot(query_head, key_head.T, preferred_element_type=jnp.float32)
        maxima = jnp.max(scores, axis=-1, keepdims=True)
        weights = jnp.exp(scores - maxima)
        probability = (weights / jnp.sum(weights, axis=-1, keepdims=True)).astype(jnp.bfloat16)
        return jnp.dot(probability, value_head, preferred_element_type=jnp.float32).astype(
            jnp.bfloat16
        )

    per_head = lax.map(
        single,
        (jnp.swapaxes(queries, 0, 1), jnp.swapaxes(key_rows, 0, 1), jnp.swapaxes(value_rows, 0, 1)),
    )
    return jnp.swapaxes(per_head, 0, 1).reshape(queries.shape[0], -1)


def slot_order(server_list):
    clip_count = server_list.shape[0]
    indices = jnp.arange(clip_count, dtype=jnp.int32)
    earlier = (server_list[None, :] < server_list[:, None]) | (
        server_list[None, :] == server_list[:, None]
    ) & (indices[None, :] < indices[:, None])
    slot_of = jnp.sum(earlier.astype(jnp.int32), axis=1)
    return jnp.sum(jnp.where(slot_of[None, :] == indices[:, None], indices[None, :], 0), axis=1)


def regroup(block_rows, clip_order):
    group_size = lax.axis_size("dp")
    piece_rows = block_rows.reshape(group_size, -1)
    shuffled = lax.all_to_all(piece_rows, "dp", split_axis=0, concat_axis=0, tiled=True)
    picked = jnp.take(shuffled, clip_order, axis=0)
    returned = lax.all_to_all(picked, "dp", split_axis=0, concat_axis=0, tiled=True)
    return returned.reshape(block_rows.shape)


def block_term(operand, weight_rows, row_count, frame_count, local_width):
    blocks = row_count // frame_count
    product = jnp.dot(operand, weight_rows, preferred_element_type=jnp.float32)
    return (
        product.reshape(frame_count, blocks, local_width)
        .transpose(1, 0, 2)
        .reshape(blocks * frame_count, local_width)
    )


def on_device(
    frames_in,
    ln1_gain,
    ln1_bias,
    qkv_weight,
    qv_bias,
    out_weight,
    out_bias,
    ln2_gain,
    ln2_bias,
    fc1_weight,
    fc1_bias,
    fc2_weight,
    fc2_bias,
    server_of_clip,
):
    clip_order = slot_order(server_of_clip)
    group_rows = frames_in.shape[2]
    local_width = frames_in.shape[3] // 4
    frame_count = group_rows * 4
    residual_in = frames_in[0, 0].reshape(frame_count, local_width)
    residual_in = regroup(residual_in, clip_order)
    normed_one = normalize(residual_in, ln1_gain, ln1_bias)
    column_count = qkv_weight.shape[2]
    weight_piece = lax.all_gather(qkv_weight, "dp", axis=0, tiled=True)
    operand = normed_one
    projected = jnp.dot(
        operand, weight_piece.reshape(weight_piece.shape[0], -1), preferred_element_type=jnp.float32
    ).reshape(frame_count, 3, column_count)
    queries = (
        ((projected[:, 0] + qv_bias[0]) * HDIM ** (-0.5))
        .astype(jnp.bfloat16)
        .reshape(frame_count, -1, HDIM)
    )
    key_rows = projected[:, 1].astype(jnp.bfloat16).reshape(frame_count, -1, HDIM)
    value_rows = (projected[:, 2] + qv_bias[1]).astype(jnp.bfloat16).reshape(frame_count, -1, HDIM)
    context = attend(queries, key_rows, value_rows)
    output_rows = lax.all_gather(out_weight, "dp", axis=0, tiled=True)
    carried = residual_in.astype(jnp.float32) + out_bias
    attended = (
        carried
        + lax.psum_scatter(
            block_term(
                context, output_rows, frame_count * lax.axis_size("head"), frame_count, local_width
            ).astype(jnp.bfloat16),
            "head",
            scatter_dimension=0,
            tiled=True,
        ).astype(jnp.float32)
    ).astype(jnp.bfloat16)
    normed_two = normalize(attended, ln2_gain, ln2_bias)
    operand = normed_two
    hidden_sums = jnp.dot(
        operand,
        lax.all_gather(fc1_weight, "dp", axis=0, tiled=True),
        preferred_element_type=jnp.float32,
    )
    hidden = jax.nn.gelu(hidden_sums + fc1_bias, approximate=False).astype(jnp.bfloat16)
    down_rows = lax.all_gather(fc2_weight, "dp", axis=0, tiled=True)
    kept = attended.astype(jnp.float32) + fc2_bias
    layer_out = (
        kept
        + lax.psum_scatter(
            block_term(
                hidden, down_rows, frame_count * lax.axis_size("head"), frame_count, local_width
            ).astype(jnp.bfloat16),
            "head",
            scatter_dimension=0,
            tiled=True,
        ).astype(jnp.float32)
    ).astype(jnp.bfloat16)
    return layer_out.reshape(1, 1, group_rows, 4 * local_width)


MESH = pl.DeviceIdType.MESH
VMEM = pltpu.MemorySpace.VMEM
ANY = pl.ANY
CORES = 2
PAIR = 2 * HDIM
UP, DOWN, SIDE, CORE = range(4)


def at_rows(index, rows):
    return pl.ds(pl.multiple_of(index * rows, rows), rows)


def norm_rows(floats, gain, shift):
    center = jnp.mean(floats, axis=-1, keepdims=True)
    moved = floats - center
    spread = jnp.mean(jnp.square(moved), axis=-1, keepdims=True)
    return (moved * lax.rsqrt(spread + epsilon) * gain + shift).astype(jnp.bfloat16)


def loop(start, stop, body):
    def step(k, carry):
        body(k)
        return carry

    lax.fori_loop(start, stop, step, 0)


class Gather:
    def __init__(self, me, h, dp, parts, send, recv):
        self.h, self.parts, self.send, self.recv = h, parts, send, recv
        self.sides = 2
        self.length = dp // (self.sides * CORES)
        self.core = lax.rem(me, CORES)
        self.side = lax.rem(lax.div(me, CORES), self.sides)
        self.z = lax.div(me, CORES * self.sides)
        self.started = []

    def index(self, z, side, core):
        return (z * self.sides + side) * CORES + core

    def copy(self, t, origin, route):
        target = {
            UP: lambda: self.index(self.z + 1, self.side, self.core),
            DOWN: lambda: self.index(self.z - 1, self.side, self.core),
            SIDE: lambda: self.index(self.z, 1 - self.side, self.core),
            CORE: lambda: self.index(self.z, self.side, 1 - self.core),
        }[route]()
        ref = self.parts[t](origin)
        return pltpu.make_async_remote_copy(
            ref, ref, self.send.at[t, route, origin], self.recv.at[t, origin], (target, self.h), MESH
        )

    def go(self, t, origin, routes, act):
        for route in routes:
            copy = self.copy(t, origin, route)
            if route == UP:
                pl.when(self.z < self.length - 1)(lambda copy=copy: act(copy))
            elif route == DOWN:
                pl.when(self.z > 0)(lambda copy=copy: act(copy))
            else:
                act(copy)

    def own(self, t, act):
        self.go(t, self.index(self.z, self.side, self.core), (UP, DOWN, SIDE, CORE), act)

    def line(self, t, s, act, arrive=True):
        @pl.when(self.z >= s)
        def _():
            origin = self.index(self.z - s, self.side, self.core)
            if arrive:
                self.copy(t, origin, CORE).wait_recv()
            self.go(t, origin, (UP, SIDE, CORE), act)

        @pl.when(self.z + s < self.length)
        def _():
            origin = self.index(self.z + s, self.side, self.core)
            if arrive:
                self.copy(t, origin, CORE).wait_recv()
            self.go(t, origin, (DOWN, SIDE, CORE), act)

    def across(self, t, s, act, arrive=True):
        def one(z):
            origin = self.index(z, 1 - self.side, self.core)
            if arrive:
                self.copy(t, origin, CORE).wait_recv()
            self.go(t, origin, (CORE,), act)

        if s == 0:
            one(self.z)
            return
        pl.when(self.z >= s)(lambda: one(self.z - s))
        pl.when(self.z + s < self.length)(lambda: one(self.z + s))

    def rest(self, t):
        def one(k):
            origin = k * CORES + 1 - self.core
            self.copy(t, origin, CORE).wait_recv()

        loop(0, self.length * self.sides, one)

    def finish(self, t):
        act = lambda copy: copy.wait_send()
        self.own(t, act)
        for s in range(1, self.length):
            self.line(t, s, act, False)
        for s in range(self.length):
            self.across(t, s, act, False)


def layer_kernel(
    dp,
    sizes,
    order_ref,
    par_ref,
    x_ref,
    wq_ref,
    wo_ref,
    w1_ref,
    w2_ref,
    o_ref,
    all_q,
    all_o,
    all_1,
    all_2,
    x,
    q,
    k,
    v,
    ctx,
    att,
    second,
    full,
    normed,
    hidden,
    out,
    got,
    kept,
    done,
    wsend,
    wrecv,
    own_sem,
    xs,
    xr,
    xo,
    os_,
    or_,
    cs,
    cr,
    s1,
    r1,
    s2,
    r2,
    s3,
    r3,
    fs,
    fr,
    ds,
    *first,
):
    start = lambda copy: copy.start()
    me, h = lax.axis_index("dp"), lax.axis_index("head")
    there = 1 - h
    peer = (me, there)
    groups = x_ref.shape[0]
    width = x_ref.shape[1] // 4
    frames, depth = x.shape
    columns = q.shape[1]
    pairs = columns // PAIR
    blocks, _, rows, _ = second.shape
    block = frames // blocks
    tile = sizes["tile"]
    chunk = sizes["chunk"]
    (g1, b1), (g2, b2), qb, vb, ob, fb, f1 = sizes["offsets"]

    def par(offset, size):
        return par_ref[0:1, offset : offset + size]

    barrier = pltpu.get_barrier_semaphore()

    def hello(n):
        pl.semaphore_signal(barrier, inc=1, device_id=(lax.rem(me + n, dp), h), device_id_type=MESH)

    loop(1, dp, hello)
    pl.semaphore_signal(barrier, inc=1, device_id=peer, device_id_type=MESH)

    parts = [
        lambda d: all_q.at[:, at_rows(d, wq_ref.shape[1]), :],
        lambda d: all_o.at[:, at_rows(d, wo_ref.shape[0]), :],
        lambda d: all_1.at[at_rows(d, w1_ref.shape[0]), :],
        lambda d: all_2.at[at_rows(d, w2_ref.shape[0]), :],
    ]
    net = Gather(me, h, dp, parts, wsend, wrecv)
    mine = [
        pltpu.make_async_copy(wq_ref, parts[0](me), own_sem.at[0]),
        pltpu.make_async_copy(
            wo_ref.at[:, at_rows(h, width)],
            all_o.at[h, at_rows(me, wo_ref.shape[0]), :],
            own_sem.at[1],
        ),
        pltpu.make_async_copy(w1_ref, parts[2](me), own_sem.at[2]),
        pltpu.make_async_copy(w2_ref, parts[3](me), own_sem.at[3]),
    ]
    for copy in mine:
        copy.start()

    def x_part(j):
        return x_ref.at[:, j * width : (j + 1) * width], x.at[
            j * groups : (j + 1) * groups, at_rows(h, width)
        ]

    for j in range(4):
        pltpu.make_async_copy(*x_part(j), xo.at[j]).start()
    mine[0].wait()
    pl.semaphore_wait(barrier, dp)

    half = pltpu.make_async_remote_copy(
        wo_ref.at[:, at_rows(there, width)],
        all_o.at[h, at_rows(me, wo_ref.shape[0]), :],
        os_,
        or_,
        peer,
        MESH,
    )
    half.start()
    net.own(0, start)

    def x_copy(j):
        source, target = x_part(j)
        return pltpu.make_async_remote_copy(source, target, xs.at[j], xr.at[j], peer, MESH)

    for j in range(4):
        x_copy(j).start()

    def out_own():
        mine[1].wait()
        half.wait_recv()
        net.own(1, start)

    def up_own():
        mine[2].wait()
        net.own(2, start)

    def down_own():
        mine[3].wait()
        net.own(3, start)

    L = lambda t, s: lambda: net.line(t, s, start)
    A = lambda t, s: lambda: net.across(t, s, start)
    for step in sizes["early"](L, A, out_own, up_own, down_own):
        step()
    later = sizes["later"](L, A, out_own, up_own, down_own)
    net.rest(0)

    def project(j):
        at = at_rows(j, groups)
        n = norm_rows(x[at, :].astype(jnp.float32), par(g1, depth), par(b1, depth))

        def part(i):
            return jnp.dot(n, all_q[i], preferred_element_type=jnp.float32)

        q[at, :] = ((part(0) + par(qb, columns)) * HDIM ** (-0.5)).astype(jnp.bfloat16)
        k[at, :] = part(1).astype(jnp.bfloat16)
        v[at, :] = (part(2) + par(vb, columns)).astype(jnp.bfloat16)

    for j in range(4):
        pltpu.make_async_copy(*x_part(j), xo.at[j]).wait()
        x_copy(j).wait_recv()

    loop(0, 4, project)

    lane = lax.broadcasted_iota(jnp.int32, (1, PAIR), 1)
    low_f = jnp.where(lane < HDIM, 1.0, 0.0)
    low, high = low_f.astype(jnp.bfloat16), (1.0 - low_f).astype(jnp.bfloat16)

    def attend(b, p):
        cols = at_rows(p, PAIR)
        keys, values = k[:, cols], v[:, cols]

        def head(query, value):
            scores = lax.dot_general(
                query, keys, (((1,), (1,)), ((), ())), preferred_element_type=jnp.float32
            )
            top = jnp.max(scores, axis=-1, keepdims=True)
            weights = jnp.exp(scores - top).astype(jnp.bfloat16)
            return jnp.dot(weights, value, preferred_element_type=jnp.float32)

        at = at_rows(b, block)
        query = q[at, cols]
        one = head(query * low, values * low + high)
        two = head(query * high, values * high + low)
        top = one * low_f + two * (1.0 - low_f)
        total = pltpu.roll(one * (1.0 - low_f) + two * low_f, HDIM, 1)
        ctx[at, at_rows(h * pairs + p, PAIR)] = (top / total).astype(jnp.bfloat16)

    def ctx_copy(b):
        ref = ctx.at[at_rows(b, block), at_rows(h, columns)]
        return pltpu.make_async_remote_copy(ref, ref, cs.at[b], cr.at[b], peer, MESH)

    def attended(b):
        ctx_copy(b).wait_recv()
        at = at_rows(b, block)
        total = x[at, at_rows(h, width)].astype(jnp.float32) + par(ob, width)
        for i in range(2):
            total = total + jnp.dot(
                ctx[at, i * columns : (i + 1) * columns],
                all_o[i],
                preferred_element_type=jnp.float32,
            )
        att[at, :] = total.astype(jnp.bfloat16)

    def piece(ref, b, j):
        return ref.at[at_rows(b * dp + j, rows)]

    def home(b, j):
        return full.at[at_rows(b * dp + j, rows), at_rows(h, width)]

    def one(b, n):
        other = lax.rem(me + n, dp)
        return pltpu.make_async_remote_copy(
            piece(att, b, other), first[b].at[me], s1.at[b, n], r1.at[b, n], (other, h), MESH
        )

    def one_own(b):
        return pltpu.make_async_copy(piece(att, b, me), first[b].at[me], r1.at[b, 0])

    def two(b, n):
        other = lax.rem(me + n, dp)
        return pltpu.make_async_remote_copy(
            second.at[b, other], home(b, me), s2.at[b, n], r2.at[b, n], (other, h), MESH
        )

    def two_own(b):
        return pltpu.make_async_copy(second.at[b, me], home(b, me), r2.at[b, 0])

    def three(b):
        ref = full.at[at_rows(b, block), at_rows(h, width)]
        return pltpu.make_async_remote_copy(ref, ref, s3.at[b], r3.at[b], peer, MESH)

    def spread(b):
        one_own(b).start()
        loop(1, dp, lambda n: one(b, n).start())

    def pick(b):
        one_own(b).wait()
        loop(1, dp, lambda n: one(b, n).wait_recv())

        def choose(s):
            second[b, s] = first[b][order_ref[s]]

        loop(0, dp, choose)
        two_own(b).start()
        loop(1, dp, lambda n: two(b, n).start())

    def forward(b):
        two_own(b).wait()
        loop(1, dp, lambda n: two(b, n).wait_recv())
        three(b).start()

    def share(target):
        return jnp.dot(
            hidden[...], all_2[:, at_rows(target, width)], preferred_element_type=jnp.float32
        )

    def out_copy(b):
        return pltpu.make_async_remote_copy(
            out.at[b], got.at[b], fs.at[b], fr.at[b], peer, MESH
        )

    def feed(b):
        three(b).wait_recv()
        at = at_rows(b, block)
        normed[...] = norm_rows(full[at, :].astype(jnp.float32), par(g2, depth), par(b2, depth))

        for t in range(hidden.shape[1] // tile):
            cols = slice(t * tile, (t + 1) * tile)
            sums = jnp.dot(normed[...], all_1[:, cols], preferred_element_type=jnp.float32)
            sums = sums + par(f1 + t * tile, tile)
            hidden[:, cols] = (0.5 * sums * (1.0 + lax.erf(sums * 0.7071067811865476))).astype(
                jnp.bfloat16
            )

        out[b] = share(there).astype(jnp.bfloat16)
        out_copy(b).start()
        kept[b] = full[at, at_rows(h, width)].astype(jnp.float32) + par(fb, width) + share(h)

    def done_copy(b, i):
        n = b * (block // chunk) + i
        per = groups // chunk
        return pltpu.make_async_copy(
            done.at[at_rows(n, chunk)],
            o_ref.at[at_rows(lax.rem(n, per), chunk), at_rows(lax.div(n, per), width)],
            ds.at[b, i],
        )

    def close(b):
        out_copy(b).wait_recv()
        done[at_rows(b, block), :] = (kept[b] + got[b].astype(jnp.float32)).astype(jnp.bfloat16)
        loop(0, block // chunk, lambda i: done_copy(b, i).start())

    def when(i, offset, body):
        b = i - offset

        @pl.when((b >= 0) & (b < blocks))
        def _():
            body(b)

    def each_static(b, body):
        for n in range(blocks):
            pl.when(b == n)(lambda n=n: body(n))

    o_out, o_pick, o_forward, o_feed, o_close = sizes["stages"]

    def master(i):
        def attend_block(b):
            def each(p):
                attend(b, p)
                for n, step in enumerate(later):
                    pl.when(b * pairs + p == n)(step)

            loop(0, pairs, each)
            ctx_copy(b).start()

        when(i, 0, attend_block)

        def out_block(b):
            pl.when(b == 0)(lambda: net.rest(1))
            attended(b)
            each_static(b, spread)

        when(i, o_out, out_block)
        when(i, o_pick, lambda b: each_static(b, pick))
        when(i, o_forward, forward)

        def feed_block(b):
            @pl.when(b == 0)
            def _():
                for step in later[blocks * pairs :]:
                    step()
                net.rest(2)
                net.rest(3)

            feed(b)

        when(i, o_feed, feed_block)
        when(i, o_close, close)

    loop(0, blocks + o_close, master)

    for t in range(4):
        net.finish(t)
    half.wait_send()
    for j in range(4):
        x_copy(j).wait_send()

    def last(b):
        ctx_copy(b).wait_send()
        three(b).wait_send()
        out_copy(b).wait_send()
        loop(1, dp, lambda n: two(b, n).wait_send())
        loop(0, block // chunk, lambda i: done_copy(b, i).wait())

    loop(0, blocks, last)
    for b in range(blocks):
        loop(1, dp, lambda n: one(b, n).wait_send())


def early(L, A, out_own, up_own, down_own):
    return [
        out_own, L(0, 1), up_own, L(1, 1), L(0, 2), A(0, 0), A(1, 0), L(1, 2), L(0, 3), A(0, 1),
        A(1, 1), L(1, 3), A(0, 2), L(2, 1), A(1, 2), down_own, A(0, 3), A(1, 3),
    ]


def later(L, A, out_own, up_own, down_own):
    return [
        A(2, 0), L(2, 2), L(2, 3), A(2, 1), L(3, 1), A(3, 0), A(2, 2), L(3, 2), A(2, 3), L(3, 3),
        A(3, 1), A(3, 2), A(3, 3),
    ]


def on_device_aligned(
    frames_in,
    ln1_gain,
    ln1_bias,
    qkv_weight,
    qv_bias,
    out_weight,
    out_bias,
    ln2_gain,
    ln2_bias,
    fc1_weight,
    fc1_bias,
    fc2_weight,
    fc2_bias,
    server_of_clip,
):
    dp, heads = lax.axis_size("dp"), lax.axis_size("head")
    groups, width = frames_in.shape[2], frames_in.shape[3] // 4
    frames, depth = groups * 4, width * heads
    rows = 16
    blocks = frames // (dp * rows)
    block = dp * rows
    columns, units = qkv_weight.shape[2], fc1_weight.shape[1]
    values = [
        ln1_gain, ln1_bias, ln2_gain, ln2_bias, qv_bias.reshape(-1), out_bias, fc2_bias, fc1_bias
    ]
    par = jnp.concatenate(values)[None]
    base = 4 * depth
    offsets = (
        (0, depth),
        (2 * depth, 3 * depth),
        base,
        base + columns,
        base + 2 * columns,
        base + 2 * columns + width,
        base + 2 * columns + 2 * width,
    )
    sizes = {
        "tile": 512,
        "chunk": 64,
        "offsets": offsets,
        "early": early,
        "later": later,
        "stages": (1, 5, 6, 7, 8),
    }
    bf16, f32 = jnp.bfloat16, jnp.float32
    dma = pltpu.SemaphoreType.DMA
    out = pl.pallas_call(
        functools.partial(layer_kernel, dp, sizes),
        out_shape=jax.ShapeDtypeStruct((groups, 4 * width), bf16),
        in_specs=[
            pl.BlockSpec(memory_space=pltpu.MemorySpace.SMEM),
            pl.BlockSpec(memory_space=VMEM),
        ]
        + [pl.BlockSpec(memory_space=ANY)] * 5,
        out_specs=pl.BlockSpec(memory_space=ANY),
        scratch_shapes=[
            pltpu.VMEM((3, depth, columns), bf16),
            pltpu.VMEM((heads, columns, width), bf16),
            pltpu.VMEM((depth, units), bf16),
            pltpu.VMEM((units, depth), bf16),
            pltpu.VMEM((frames, depth), bf16),
            pltpu.VMEM((frames, columns), bf16),
            pltpu.VMEM((frames, columns), bf16),
            pltpu.VMEM((frames, columns), bf16),
            pltpu.VMEM((frames, heads * columns), bf16),
            pltpu.VMEM((frames, width), bf16),
            pltpu.VMEM((blocks, dp, rows, width), bf16),
            pltpu.VMEM((frames, depth), bf16),
            pltpu.VMEM((block, depth), bf16),
            pltpu.VMEM((block, units), bf16),
            pltpu.VMEM((blocks, block, width), bf16),
            pltpu.VMEM((blocks, block, width), bf16),
            pltpu.VMEM((blocks, block, width), f32),
            pltpu.VMEM((frames, width), bf16),
            dma((4, 4, dp)),
            dma((4, dp)),
            dma((4,)),
            dma((4,)),
            dma((4,)),
            dma((4,)),
            dma,
            dma,
            dma((blocks,)),
            dma((blocks,)),
            dma((blocks, dp)),
            dma((blocks, dp)),
            dma((blocks, dp)),
            dma((blocks, dp)),
            dma((blocks,)),
            dma((blocks,)),
            dma((blocks,)),
            dma((blocks,)),
            dma((blocks, block // sizes["chunk"])),
        ]
        + [pltpu.VMEM((dp, rows, width), bf16)] * blocks,
        compiler_params=pltpu.CompilerParams(
            collective_id=0, has_side_effects=True, vmem_limit_bytes=66000000
        ),
        name="layer",
    )(
        slot_order(server_of_clip),
        par,
        frames_in[0, 0],
        jnp.swapaxes(qkv_weight, 0, 1),
        out_weight,
        fc1_weight,
        fc2_weight,
    )
    return out[None, None]


def aligned(mesh, frames_in, qkv_weight, out_weight, fc1_weight):
    dp, heads = mesh.shape["dp"], mesh.shape["head"]
    groups, width = frames_in.shape[2], frames_in.shape[3] // 4
    frames = groups * 4
    return (
        dp % 4 == 0
        and dp >= 16
        and heads == 2
        and frames % (dp * 16) == 0
        and groups % 64 == 0
        and (dp * 16) % 64 == 0
        and width % 128 == 0
        and out_weight.shape[0] % (dp * heads * 16) == 0
        and (qkv_weight.shape[2] // heads) % PAIR == 0
        and (qkv_weight.shape[0] // dp) % 16 == 0
        and (fc1_weight.shape[1] // heads) % 512 == 0
    )


def solution(mesh):
    placed = (
        P("dp", "head", None, None),
        P(),
        P(),
        P("dp", None, "head"),
        P(None, "head"),
        P(("head", "dp"), None),
        P("head"),
        P(),
        P(),
        P("dp", "head"),
        P("head"),
        P(("head", "dp"), None),
        P("head"),
        P(),
    )

    def layer(*args):
        body = on_device_aligned if aligned(mesh, args[0], args[3], args[5], args[9]) else on_device
        return jax.shard_map(
            body,
            mesh=mesh,
            in_specs=placed,
            out_specs=P("dp", "head", None, None),
            check_vma=False,
        )(*args)

    return layer
```

time: 330 us -> 245 us (0.74); the launches traced: 326 us -> 244 us
  Pallas kernels: 270 us -> 234 us
  waiting for transfers between devices: 19.9 us -> 0 us
  between operations: 13.2 us -> 0.02 us
  local copies, waits for them, and re-layouts: 17.3 us -> 8.95 us
  blocking collectives: 3.53 us -> 0 us
    pallas_call x5 -> x1, Pallas kernels: 270 us -> 234 us  [on_device_aligned(): pl.pallas_call(functools.partial(layer_kernel, dp, sizes), out_shape=jax....]
    all_gather x3 -> x0, waiting for transfers between devices: 18.5 us -> none  [the longest x1 18.5 us: on_device_aligned(): w_down = lax.all_gather(fc2_weight, 'dp', axis=0, tiled=True)]
    broadcast_in_dim x6 -> x1, local copies, waits for them, and re-layouts: 5.38 us -> 0.64 us  [on_device_aligned(): par = jnp.concatenate(values)[None]]
    all_gather x1 -> x0, blocking collectives: 3.53 us -> none  [on_device_aligned(): whole_bias = lax.all_gather(out_bias, 'head', axis=0, tiled=True)]
    unnamed x14 -> x9, local copies, waits for them, and re-layouts: 10.3 us -> 7.59 us
  transfers between devices with their start and end apart: 3 -> 0, of which waited for: 1 -> 0; matrix products, arithmetic and copies ran while one was open for 2% -> 0% of each run, Pallas kernels for 68% -> 0%
where the time goes in v1:
time: 245 us; the launch traced here: 244 us
  Pallas kernels  234 us (96%)
  local copies, waits for them, and re-layouts  8.95 us (4%)
    pallas_call x1, Pallas kernels, on_device_aligned(): pl.pallas_call(functools.partial(layer_kernel, dp, sizes), out_shape=jax....  234 us
    unnamed x9, local copies, waits for them, and re-layouts  7.59 us

profile of v1, /device:TPU:27, one launch (start us, length us, event | category | flops | bytes accessed | tf_op | source)
XLA Modules:
  0.0 244.0 jit_solution(12733467086397081177)
XLA Ops:
  0.0 0.9 convert_reduce_fusion
  0.9 0.6 select_reduce_fusion.order_ref
  1.5 0.7 copy.15
  2.2 0.7 constant_dynamic-update-slice_fusion.7
  2.9 0.7 constant_dynamic-update-slice_fusion.6
  3.6 0.7 constant_dynamic-update-slice_fusion.5
  4.3 0.7 constant_dynamic-update-slice_fusion.4
  5.0 0.7 constant_dynamic-update-slice_fusion.2
  5.7 0.7 constant_dynamic-update-slice_fusion.1
  6.4 0.7 constant_dynamic-update-slice_fusion
  7.1 0.6 broadcast_in_dim.11.par_ref
  7.8 233.5 %layer.1 = bf16[320,2560]{1,0:T(8,128)(2,1)} custom-call(s32[16]{0:T(128)} %select_reduce_fusion.order_ref, f32[1,9984]{1,0:T(1,128)} %broadcast_in_dim.11.par_ref, bf16[320,2560]{1,0:T(8,128)(2,1)} %bitcast.6, bf16[3,80,512]{2,1,0:T(8,128)(2,1)} %bitcast.7, bf16[32,1280]{1,0:T(8,128)(2,1)} %wo_ref.1, bf16[80,2560]{1,0:T(8,128)(2,1)} %w1_ref.1, ...), custom_call_target="tpu_custom_call" | custom-call | tf_op jit(solution)/shard_map/layer/pallas_call | solution.py:679
  241.3 2.7 %copy.25 = bf16[1,1,320,2560]{3,2,1,0:T(8,128)(2,1)} copy(bf16[1,1,320,2560]{3,2,1,0:T(8,128)(2,1)} %bitcast.5) | data formatting | bytes 3276800
  (2 shorter events, 0.0 us)

commit v2 on v1

--- a/solution.py
+++ b/solution.py
@@ -211,8 +211,8 @@
             else:
                 act(copy)
 
-    def own(self, t, act):
-        self.go(t, self.index(self.z, self.side, self.core), (UP, DOWN, SIDE, CORE), act)
+    def own(self, t, act, routes=(UP, DOWN, SIDE, CORE)):
+        self.go(t, self.index(self.z, self.side, self.core), routes, act)
 
     def line(self, t, s, act, arrive=True):
         @pl.when(self.z >= s)
@@ -242,6 +242,23 @@
         pl.when(self.z >= s)(lambda: one(self.z - s))
         pl.when(self.z + s < self.length)(lambda: one(self.z + s))
 
+    def twin(self, t, act, arrive=True):
+        origin = self.index(self.z, 1 - self.side, self.core)
+        if arrive:
+            self.copy(t, origin, CORE).wait_recv()
+        self.go(t, origin, (UP, DOWN, CORE), act)
+
+    def both(self, t, s, act, arrive=True):
+        def one(z, route):
+            for side in range(self.sides):
+                origin = self.index(z, side, self.core)
+                if arrive:
+                    self.copy(t, origin, CORE).wait_recv()
+                self.go(t, origin, (route, CORE), act)
+
+        pl.when(self.z >= s)(lambda: one(self.z - s, UP))
+        pl.when(self.z + s < self.length)(lambda: one(self.z + s, DOWN))
+
     def rest(self, t):
         def one(k):
             origin = k * CORES + 1 - self.core
@@ -249,9 +266,14 @@
 
         loop(0, self.length * self.sides, one)
 
-    def finish(self, t):
+    def finish(self, t, paired):
         act = lambda copy: copy.wait_send()
         self.own(t, act)
+        if paired:
+            self.twin(t, act, False)
+            for s in range(1, self.length):
+                self.both(t, s, act, False)
+            return
         for s in range(1, self.length):
             self.line(t, s, act, False)
         for s in range(self.length):
@@ -262,7 +284,36 @@
     dp,
     sizes,
     order_ref,
+    *refs,
+):
+    count = len(sizes["lengths"])
+    values, refs = refs[:count], refs[count:]
+    par_ref, par_sem, flat, refs = refs[-2 - count], refs[-1], refs[-1 - count : -1], refs[: -2 - count]
+    copies = [
+        pltpu.make_async_copy(value, part, par_sem.at[n])
+        for n, (value, part) in enumerate(zip(values, flat))
+    ]
+    for copy in copies:
+        copy.start()
+
+    def fill():
+        offset = 0
+        for copy, part, length in zip(copies, flat, sizes["lengths"]):
+            copy.wait()
+            for row in range(part.shape[0] if len(part.shape) == 2 else 1):
+                line = part[row : row + 1, :] if len(part.shape) == 2 else part[...][None, :]
+                par_ref[0:1, offset : offset + length] = line
+                offset += length
+
+    layer_body(dp, sizes, order_ref, par_ref, fill, *refs)
+
+
+def layer_body(
+    dp,
+    sizes,
+    order_ref,
     par_ref,
+    fill,
     x_ref,
     wq_ref,
     wo_ref,
@@ -287,6 +338,7 @@
     got,
     kept,
     done,
+    placed,
     wsend,
     wrecv,
     own_sem,
@@ -306,7 +358,6 @@
     fs,
     fr,
     ds,
-    *first,
 ):
     start = lambda copy: copy.start()
     me, h = lax.axis_index("dp"), lax.axis_index("head")
@@ -362,6 +413,7 @@
     for j in range(4):
         pltpu.make_async_copy(*x_part(j), xo.at[j]).start()
     mine[0].wait()
+    mine[2].wait()
     pl.semaphore_wait(barrier, dp)
 
     half = pltpu.make_async_remote_copy(
@@ -387,19 +439,31 @@
         half.wait_recv()
         net.own(1, start)
 
+    def out_twin():
+        net.twin(1, start)
+
+    def up_side():
+        net.own(2, start, (SIDE,))
+
     def up_own():
-        mine[2].wait()
-        net.own(2, start)
+        net.own(2, start, (UP, DOWN, CORE))
 
     def down_own():
         mine[3].wait()
-        net.own(3, start)
+        net.own(3, start, (UP, DOWN, CORE))
+
+    def down_side():
+        net.own(3, start, (SIDE,))
 
     L = lambda t, s: lambda: net.line(t, s, start)
     A = lambda t, s: lambda: net.across(t, s, start)
-    for step in sizes["early"](L, A, out_own, up_own, down_own):
+    B = lambda t, s: lambda: net.both(t, s, start)
+    own = (out_own, out_twin, up_side, up_own, down_own, down_side)
+    before, during, after = sizes["plan"](L, A, B, own)
+    for n, step in enumerate(before):
         step()
-    later = sizes["later"](L, A, out_own, up_own, down_own)
+        if n == 1:
+            fill()
     net.rest(0)
 
     def project(j):
@@ -413,11 +477,16 @@
         k[at, :] = part(1).astype(jnp.bfloat16)
         v[at, :] = (part(2) + par(vb, columns)).astype(jnp.bfloat16)
 
-    for j in range(4):
+    def x_wait(j):
         pltpu.make_async_copy(*x_part(j), xo.at[j]).wait()
         x_copy(j).wait_recv()
 
-    loop(0, 4, project)
+    def project_when_here(j):
+        for n in range(4):
+            pl.when(j == n)(lambda n=n: x_wait(n))
+        project(j)
+
+    loop(0, 4, project_when_here)
 
     lane = lax.broadcasted_iota(jnp.int32, (1, PAIR), 1)
     low_f = jnp.where(lane < HDIM, 1.0, 0.0)
@@ -443,12 +512,12 @@
         total = pltpu.roll(one * (1.0 - low_f) + two * low_f, HDIM, 1)
         ctx[at, at_rows(h * pairs + p, PAIR)] = (top / total).astype(jnp.bfloat16)
 
-    def ctx_copy(b):
-        ref = ctx.at[at_rows(b, block), at_rows(h, columns)]
-        return pltpu.make_async_remote_copy(ref, ref, cs.at[b], cr.at[b], peer, MESH)
+    def ctx_copy(b, p):
+        ref = ctx.at[at_rows(b, block), at_rows(h * pairs + p, PAIR)]
+        return pltpu.make_async_remote_copy(ref, ref, cs.at[b, p], cr.at[b, p], peer, MESH)
 
     def attended(b):
-        ctx_copy(b).wait_recv()
+        loop(0, pairs, lambda p: ctx_copy(b, p).wait_recv())
         at = at_rows(b, block)
         total = x[at, at_rows(h, width)].astype(jnp.float32) + par(ob, width)
         for i in range(2):
@@ -468,20 +537,20 @@
     def one(b, n):
         other = lax.rem(me + n, dp)
         return pltpu.make_async_remote_copy(
-            piece(att, b, other), first[b].at[me], s1.at[b, n], r1.at[b, n], (other, h), MESH
+            piece(att, b, other), home(b, me), s1.at[b, n], r1.at[b, n], (other, h), MESH
         )
 
     def one_own(b):
-        return pltpu.make_async_copy(piece(att, b, me), first[b].at[me], r1.at[b, 0])
+        return pltpu.make_async_copy(piece(att, b, me), home(b, me), r1.at[b, 0])
 
     def two(b, n):
         other = lax.rem(me + n, dp)
         return pltpu.make_async_remote_copy(
-            second.at[b, other], home(b, me), s2.at[b, n], r2.at[b, n], (other, h), MESH
+            second.at[b, other], piece(placed, b, me), s2.at[b, n], r2.at[b, n], (other, h), MESH
         )
 
     def two_own(b):
-        return pltpu.make_async_copy(second.at[b, me], home(b, me), r2.at[b, 0])
+        return pltpu.make_async_copy(second.at[b, me], piece(placed, b, me), r2.at[b, 0])
 
     def three(b):
         ref = full.at[at_rows(b, block), at_rows(h, width)]
@@ -491,20 +560,9 @@
         one_own(b).start()
         loop(1, dp, lambda n: one(b, n).start())
 
-    def pick(b):
+    def arrive(b):
         one_own(b).wait()
         loop(1, dp, lambda n: one(b, n).wait_recv())
-
-        def choose(s):
-            second[b, s] = first[b][order_ref[s]]
-
-        loop(0, dp, choose)
-        two_own(b).start()
-        loop(1, dp, lambda n: two(b, n).start())
-
-    def forward(b):
-        two_own(b).wait()
-        loop(1, dp, lambda n: two(b, n).wait_recv())
         three(b).start()
 
     def share(target):
@@ -538,14 +596,26 @@
         n = b * (block // chunk) + i
         per = groups // chunk
         return pltpu.make_async_copy(
-            done.at[at_rows(n, chunk)],
+            placed.at[at_rows(n, chunk)],
             o_ref.at[at_rows(lax.rem(n, per), chunk), at_rows(lax.div(n, per), width)],
             ds.at[b, i],
         )
 
     def close(b):
         out_copy(b).wait_recv()
-        done[at_rows(b, block), :] = (kept[b] + got[b].astype(jnp.float32)).astype(jnp.bfloat16)
+        total = (kept[b] + got[b].astype(jnp.float32)).astype(jnp.bfloat16)
+        done[...] = total.reshape(dp, rows, width)
+
+        def choose(s):
+            second[b, s] = done[order_ref[s]]
+
+        loop(0, dp, choose)
+        two_own(b).start()
+        loop(1, dp, lambda n: two(b, n).start())
+
+    def store(b):
+        two_own(b).wait()
+        loop(1, dp, lambda n: two(b, n).wait_recv())
         loop(0, block // chunk, lambda i: done_copy(b, i).start())
 
     def when(i, offset, body):
@@ -555,38 +625,39 @@
         def _():
             body(b)
 
-    def each_static(b, body):
-        for n in range(blocks):
-            pl.when(b == n)(lambda n=n: body(n))
-
-    o_out, o_pick, o_forward, o_feed, o_close = sizes["stages"]
+    o_out, o_arrive, o_feed, o_close, o_store = sizes["stages"]
+
+    def run(table, at):
+        for n, steps in table.items():
+
+            @pl.when(at == n)
+            def _(steps=steps):
+                for step in steps:
+                    step()
 
     def master(i):
         def attend_block(b):
             def each(p):
                 attend(b, p)
-                for n, step in enumerate(later):
-                    pl.when(b * pairs + p == n)(step)
+                ctx_copy(b, p).start()
+                run(during, b * pairs + p)
 
             loop(0, pairs, each)
-            ctx_copy(b).start()
 
         when(i, 0, attend_block)
 
         def out_block(b):
             pl.when(b == 0)(lambda: net.rest(1))
             attended(b)
-            each_static(b, spread)
+            spread(b)
 
         when(i, o_out, out_block)
-        when(i, o_pick, lambda b: each_static(b, pick))
-        when(i, o_forward, forward)
+        run(after, i)
+        when(i, o_arrive, arrive)
 
         def feed_block(b):
             @pl.when(b == 0)
             def _():
-                for step in later[blocks * pairs :]:
-                    step()
                 net.rest(2)
                 net.rest(3)
 
@@ -594,39 +665,39 @@
 
         when(i, o_feed, feed_block)
         when(i, o_close, close)
-
-    loop(0, blocks + o_close, master)
+        when(i, o_store, store)
+
+    loop(0, blocks + o_store, master)
 
     for t in range(4):
-        net.finish(t)
+        net.finish(t, t == 1)
     half.wait_send()
     for j in range(4):
         x_copy(j).wait_send()
 
     def last(b):
-        ctx_copy(b).wait_send()
+        loop(0, pairs, lambda p: ctx_copy(b, p).wait_send())
         three(b).wait_send()
         out_copy(b).wait_send()
+        loop(1, dp, lambda n: one(b, n).wait_send())
         loop(1, dp, lambda n: two(b, n).wait_send())
         loop(0, block // chunk, lambda i: done_copy(b, i).wait())
 
     loop(0, blocks, last)
-    for b in range(blocks):
-        loop(1, dp, lambda n: one(b, n).wait_send())
-
-
-def early(L, A, out_own, up_own, down_own):
-    return [
-        out_own, L(0, 1), up_own, L(1, 1), L(0, 2), A(0, 0), A(1, 0), L(1, 2), L(0, 3), A(0, 1),
-        A(1, 1), L(1, 3), A(0, 2), L(2, 1), A(1, 2), down_own, A(0, 3), A(1, 3),
+
+
+def plan(L, A, B, own):
+    out_own, out_twin, up_side, up_own, down_own, down_side = own
+    before = [
+        out_own, up_side, L(0, 1), out_twin, B(1, 1), L(0, 2), up_own, A(0, 0), A(0, 1), B(1, 2),
+        L(0, 3), down_own, A(0, 2), B(1, 3), down_side, L(2, 1), A(0, 3),
     ]
-
-
-def later(L, A, out_own, up_own, down_own):
-    return [
-        A(2, 0), L(2, 2), L(2, 3), A(2, 1), L(3, 1), A(3, 0), A(2, 2), L(3, 2), A(2, 3), L(3, 3),
-        A(3, 1), A(3, 2), A(3, 3),
-    ]
+    during = {0: [L(3, 1)], 8: [L(2, 2)], 14: [L(3, 2)]}
+    after = {
+        4: [L(2, 3)], 5: [L(3, 3), A(2, 0), A(3, 0), A(2, 1)], 6: [A(3, 1), A(2, 2)],
+        7: [A(3, 2)], 8: [A(2, 3), A(3, 3)],
+    }
+    return before, during, after
 
 
 def on_device_aligned(
@@ -653,9 +724,8 @@
     block = dp * rows
     columns, units = qkv_weight.shape[2], fc1_weight.shape[1]
     values = [
-        ln1_gain, ln1_bias, ln2_gain, ln2_bias, qv_bias.reshape(-1), out_bias, fc2_bias, fc1_bias
+        ln1_gain, ln1_bias, ln2_gain, ln2_bias, qv_bias, out_bias, fc2_bias, fc1_bias
     ]
-    par = jnp.concatenate(values)[None]
     base = 4 * depth
     offsets = (
         (0, depth),
@@ -670,9 +740,9 @@
         "tile": 512,
         "chunk": 64,
         "offsets": offsets,
-        "early": early,
-        "later": later,
-        "stages": (1, 5, 6, 7, 8),
+        "lengths": [value.shape[-1] for value in values],
+        "plan": plan,
+        "stages": (1, 4, 8, 10, 12),
     }
     bf16, f32 = jnp.bfloat16, jnp.float32
     dma = pltpu.SemaphoreType.DMA
@@ -681,9 +751,8 @@
         out_shape=jax.ShapeDtypeStruct((groups, 4 * width), bf16),
         in_specs=[
             pl.BlockSpec(memory_space=pltpu.MemorySpace.SMEM),
-            pl.BlockSpec(memory_space=VMEM),
         ]
-        + [pl.BlockSpec(memory_space=ANY)] * 5,
+        + [pl.BlockSpec(memory_space=ANY)] * (5 + len(values)),
         out_specs=pl.BlockSpec(memory_space=ANY),
         scratch_shapes=[
             pltpu.VMEM((3, depth, columns), bf16),
@@ -703,6 +772,7 @@
             pltpu.VMEM((blocks, block, width), bf16),
             pltpu.VMEM((blocks, block, width), bf16),
             pltpu.VMEM((blocks, block, width), f32),
+            pltpu.VMEM((dp, rows, width), bf16),
             pltpu.VMEM((frames, width), bf16),
             dma((4, 4, dp)),
             dma((4, dp)),
@@ -712,8 +782,8 @@
             dma((4,)),
             dma,
             dma,
-            dma((blocks,)),
-            dma((blocks,)),
+            dma((blocks, columns // PAIR)),
+            dma((blocks, columns // PAIR)),
             dma((blocks, dp)),
             dma((blocks, dp)),
             dma((blocks, dp)),
@@ -723,15 +793,17 @@
             dma((blocks,)),
             dma((blocks,)),
             dma((blocks, block // sizes["chunk"])),
-        ]
-        + [pltpu.VMEM((dp, rows, width), bf16)] * blocks,
+            pltpu.VMEM((1, sum(value.size for value in values)), f32),
+            *[pltpu.VMEM(value.shape, f32) for value in values],
+            dma((len(values),)),
+        ],
         compiler_params=pltpu.CompilerParams(
             collective_id=0, has_side_effects=True, vmem_limit_bytes=66000000
         ),
         name="layer",
     )(
         slot_order(server_of_clip),
-        par,
+        *values,
         frames_in[0, 0],
         jnp.swapaxes(qkv_weight, 0, 1),
         out_weight,

time: 245 us -> 196 us (0.80)
  Pallas kernels: 234 us -> 190 us
  local copies, waits for them, and re-layouts: 8.95 us -> 2.7 us
    pallas_call x1, Pallas kernels: 234 us -> 190 us  [on_device_aligned(): pl.pallas_call(functools.partial(layer_kernel, dp, sizes), out_shape=jax....]
    unnamed x9 -> x1, local copies, waits for them, and re-layouts: 7.59 us -> 2.7 us
where the time goes in v2:
time: 196 us; the launch traced here: 195 us
  Pallas kernels  190 us (97%)
  local copies, waits for them, and re-layouts  2.7 us (1%)
    pallas_call x1, Pallas kernels, on_device_aligned(): pl.pallas_call(functools.partial(layer_kernel, dp, sizes), out_shape=jax....  190 us

profile of v2, /device:TPU:27, one launch (start us, length us, event | category | flops | bytes accessed | tf_op | source)
XLA Modules:
  0.0 194.7 jit_solution(17887489397020876956)
XLA Ops:
  0.0 0.9 convert_reduce_fusion
  0.9 0.6 select_reduce_fusion.order_ref
  1.5 190.4 %layer.1 = bf16[320,2560]{1,0:T(8,128)(2,1)} custom-call(s32[16]{0:T(128)} %select_reduce_fusion.order_ref, f32[1280]{0:T(1024)} %refs_0_.1, f32[1280]{0:T(1024)} %refs_1_.1, f32[1280]{0:T(1024)} %refs_2_.1, f32[1280]{0:T(1024)} %refs_3_.1, f32[2,512]{1,0:T(2,128)} %refs_4_.1, f32[640]{0:T(1024)} %refs_5_.1, f32[640]{0:T(1024)} %refs_6_.1, f32[2560]{0:T(1024)} %refs_7_.1, ...), custom_call_target="tpu_custom_call" | custom-call | tf_op jit(solution)/shard_map/layer/pallas_call | solution.py:749
  192.0 2.7 %copy.16 = bf16[1,1,320,2560]{3,2,1,0:T(8,128)(2,1)} copy(bf16[1,1,320,2560]{3,2,1,0:T(8,128)(2,1)} %bitcast.3) | data formatting | bytes 3276800

commit v3 on v2

--- a/solution.py
+++ b/solution.py
@@ -336,7 +336,6 @@
     hidden,
     out,
     got,
-    kept,
     done,
     placed,
     wsend,
@@ -366,7 +365,7 @@
     groups = x_ref.shape[0]
     width = x_ref.shape[1] // 4
     frames, depth = x.shape
-    columns = q.shape[1]
+    columns, units = q.shape[1], w1_ref.shape[1]
     pairs = columns // PAIR
     blocks, _, rows, _ = second.shape
     block = frames // blocks
@@ -388,8 +387,10 @@
     parts = [
         lambda d: all_q.at[:, at_rows(d, wq_ref.shape[1]), :],
         lambda d: all_o.at[:, at_rows(d, wo_ref.shape[0]), :],
-        lambda d: all_1.at[at_rows(d, w1_ref.shape[0]), :],
-        lambda d: all_2.at[at_rows(d, w2_ref.shape[0]), :],
+        lambda d: all_1.at[at_rows(d, w1_ref.shape[0]), : units // 2],
+        lambda d: all_1.at[at_rows(d, w1_ref.shape[0]), units // 2 :],
+        lambda d: all_2.at[at_rows(d, w2_ref.shape[0]), at_rows(there, width)],
+        lambda d: all_2.at[at_rows(d, w2_ref.shape[0]), at_rows(h, width)],
     ]
     net = Gather(me, h, dp, parts, wsend, wrecv)
     mine = [
@@ -399,8 +400,8 @@
             all_o.at[h, at_rows(me, wo_ref.shape[0]), :],
             own_sem.at[1],
         ),
-        pltpu.make_async_copy(w1_ref, parts[2](me), own_sem.at[2]),
-        pltpu.make_async_copy(w2_ref, parts[3](me), own_sem.at[3]),
+        pltpu.make_async_copy(w1_ref, all_1.at[at_rows(me, w1_ref.shape[0]), :], own_sem.at[2]),
+        pltpu.make_async_copy(w2_ref, all_2.at[at_rows(me, w2_ref.shape[0]), :], own_sem.at[3]),
     ]
     for copy in mine:
         copy.start()
@@ -412,8 +413,8 @@
 
     for j in range(4):
         pltpu.make_async_copy(*x_part(j), xo.at[j]).start()
-    mine[0].wait()
-    mine[2].wait()
+    for n in (0, 2, 3):
+        mine[n].wait()
     pl.semaphore_wait(barrier, dp)
 
     half = pltpu.make_async_remote_copy(
@@ -442,24 +443,12 @@
     def out_twin():
         net.twin(1, start)
 
-    def up_side():
-        net.own(2, start, (SIDE,))
-
-    def up_own():
-        net.own(2, start, (UP, DOWN, CORE))
-
-    def down_own():
-        mine[3].wait()
-        net.own(3, start, (UP, DOWN, CORE))
-
-    def down_side():
-        net.own(3, start, (SIDE,))
-
     L = lambda t, s: lambda: net.line(t, s, start)
     A = lambda t, s: lambda: net.across(t, s, start)
     B = lambda t, s: lambda: net.both(t, s, start)
-    own = (out_own, out_twin, up_side, up_own, down_own, down_side)
-    before, during, after = sizes["plan"](L, A, B, own)
+    S = lambda t: lambda: net.own(t, start, (SIDE,))
+    U = lambda t: lambda: net.own(t, start, (UP, DOWN, CORE))
+    before, during, after = sizes["plan"](L, A, B, S, U, out_own, out_twin)
     for n, step in enumerate(before):
         step()
         if n == 1:
@@ -565,9 +554,11 @@
         loop(1, dp, lambda n: one(b, n).wait_recv())
         three(b).start()
 
-    def share(target):
+    def share(b, target):
         return jnp.dot(
-            hidden[...], all_2[:, at_rows(target, width)], preferred_element_type=jnp.float32
+            hidden[at_rows(b, block), :],
+            all_2[:, at_rows(target, width)],
+            preferred_element_type=jnp.float32,
         )
 
     def out_copy(b):
@@ -580,17 +571,16 @@
         at = at_rows(b, block)
         normed[...] = norm_rows(full[at, :].astype(jnp.float32), par(g2, depth), par(b2, depth))
 
-        for t in range(hidden.shape[1] // tile):
+        for t in range(units // tile):
             cols = slice(t * tile, (t + 1) * tile)
             sums = jnp.dot(normed[...], all_1[:, cols], preferred_element_type=jnp.float32)
             sums = sums + par(f1 + t * tile, tile)
-            hidden[:, cols] = (0.5 * sums * (1.0 + lax.erf(sums * 0.7071067811865476))).astype(
+            hidden[at, cols] = (0.5 * sums * (1.0 + lax.erf(sums * 0.7071067811865476))).astype(
                 jnp.bfloat16
             )
 
-        out[b] = share(there).astype(jnp.bfloat16)
+        out[b] = share(b, there).astype(jnp.bfloat16)
         out_copy(b).start()
-        kept[b] = full[at, at_rows(h, width)].astype(jnp.float32) + par(fb, width) + share(h)
 
     def done_copy(b, i):
         n = b * (block // chunk) + i
@@ -602,8 +592,10 @@
         )
 
     def close(b):
+        at = at_rows(b, block)
+        kept = full[at, at_rows(h, width)].astype(jnp.float32) + par(fb, width) + share(b, h)
         out_copy(b).wait_recv()
-        total = (kept[b] + got[b].astype(jnp.float32)).astype(jnp.bfloat16)
+        total = (kept + got[b].astype(jnp.float32)).astype(jnp.bfloat16)
         done[...] = total.reshape(dp, rows, width)
 
         def choose(s):
@@ -625,7 +617,7 @@
         def _():
             body(b)
 
-    o_out, o_arrive, o_feed, o_close, o_store = sizes["stages"]
+    o_arrive, o_feed, o_close, o_store = sizes["stages"]
 
     def run(table, at):
         for n, steps in table.items():
@@ -635,67 +627,82 @@
                 for step in steps:
                     step()
 
+    def sent():
+        half.wait_send()
+        for j in range(4):
+            x_copy(j).wait_send()
+
+        def block_sent(b):
+            loop(0, pairs, lambda p: ctx_copy(b, p).wait_send())
+            loop(1, dp, lambda n: one(b, n).wait_send())
+
+        loop(0, blocks, block_sent)
+        for t in range(5):
+            net.finish(t, t == 1)
+
     def master(i):
+        def out_block(b):
+            pl.when(b == 0)(lambda: net.rest(1))
+            attended(b)
+            spread(b)
+
         def attend_block(b):
             def each(p):
                 attend(b, p)
                 ctx_copy(b, p).start()
+                pl.when((p == 1) & (b > 0))(lambda: out_block(b - 1))
                 run(during, b * pairs + p)
 
             loop(0, pairs, each)
 
         when(i, 0, attend_block)
-
-        def out_block(b):
-            pl.when(b == 0)(lambda: net.rest(1))
-            attended(b)
-            spread(b)
-
-        when(i, o_out, out_block)
+        pl.when(i == blocks)(lambda: out_block(blocks - 1))
         run(after, i)
         when(i, o_arrive, arrive)
 
         def feed_block(b):
             @pl.when(b == 0)
             def _():
-                net.rest(2)
-                net.rest(3)
+                for t in (2, 3, 4):
+                    net.rest(t)
 
             feed(b)
 
         when(i, o_feed, feed_block)
-        when(i, o_close, close)
+
+        def close_block(b):
+            pl.when(b == 0)(lambda: net.rest(5))
+            close(b)
+            pl.when(b == 0)(sent)
+            pl.when(b == 1)(lambda: net.finish(5, False))
+
+        when(i, o_close, close_block)
         when(i, o_store, store)
 
     loop(0, blocks + o_store, master)
 
-    for t in range(4):
-        net.finish(t, t == 1)
-    half.wait_send()
-    for j in range(4):
-        x_copy(j).wait_send()
-
     def last(b):
-        loop(0, pairs, lambda p: ctx_copy(b, p).wait_send())
         three(b).wait_send()
         out_copy(b).wait_send()
-        loop(1, dp, lambda n: one(b, n).wait_send())
         loop(1, dp, lambda n: two(b, n).wait_send())
         loop(0, block // chunk, lambda i: done_copy(b, i).wait())
 
     loop(0, blocks, last)
 
 
-def plan(L, A, B, own):
-    out_own, out_twin, up_side, up_own, down_own, down_side = own
+def plan(L, A, B, S, U, out_own, out_twin):
     before = [
-        out_own, up_side, L(0, 1), out_twin, B(1, 1), L(0, 2), up_own, A(0, 0), A(0, 1), B(1, 2),
-        L(0, 3), down_own, A(0, 2), B(1, 3), down_side, L(2, 1), A(0, 3),
+        out_own, S(2), L(0, 1), out_twin, B(1, 1), U(2), L(0, 2), S(3), A(0, 0), A(0, 1), B(1, 2),
+        U(3), L(0, 3), S(4), U(4), A(0, 2), L(2, 1), A(0, 3),
     ]
-    during = {0: [L(3, 1)], 8: [L(2, 2)], 14: [L(3, 2)]}
+    during = {
+        0: [L(3, 1)], 1: [B(1, 3)], 2: [L(4, 1)], 6: [L(2, 2)], 10: [L(3, 2)], 14: [L(4, 2)],
+        18: [L(2, 3)],
+    }
     after = {
-        4: [L(2, 3)], 5: [L(3, 3), A(2, 0), A(3, 0), A(2, 1)], 6: [A(3, 1), A(2, 2)],
-        7: [A(3, 2)], 8: [A(2, 3), A(3, 3)],
+        4: [S(5), U(5)], 5: [L(3, 3), A(2, 0), A(3, 0), A(4, 0), A(2, 1), A(3, 1), A(4, 1)],
+        6: [L(4, 3), L(5, 1), A(2, 2), A(3, 2), A(4, 2), A(2, 3), A(3, 3)], 7: [L(5, 2), A(4, 3)],
+        8: [L(5, 3), A(5, 0)], 9: [A(5, 1)], 10: [A(5, 2)], 11: [A(5, 3)],
     }
     return before, during, after
 
@@ -742,7 +749,7 @@
         "offsets": offsets,
         "lengths": [value.shape[-1] for value in values],
         "plan": plan,
-        "stages": (1, 4, 8, 10, 12),
+        "stages": (2, 7, 12, 14),
     }
     bf16, f32 = jnp.bfloat16, jnp.float32
     dma = pltpu.SemaphoreType.DMA
@@ -768,14 +775,13 @@
             pltpu.VMEM((blocks, dp, rows, width), bf16),
             pltpu.VMEM((frames, depth), bf16),
             pltpu.VMEM((block, depth), bf16),
-            pltpu.VMEM((block, units), bf16),
+            pltpu.VMEM((frames, units), bf16),
             pltpu.VMEM((blocks, block, width), bf16),
             pltpu.VMEM((blocks, block, width), bf16),
-            pltpu.VMEM((blocks, block, width), f32),
             pltpu.VMEM((dp, rows, width), bf16),
             pltpu.VMEM((frames, width), bf16),
-            dma((4, 4, dp)),
-            dma((4, dp)),
+            dma((6, 4, dp)),
+            dma((6, dp)),
             dma((4,)),
             dma((4,)),
             dma((4,)),

time: 196 us -> 186 us (0.949)
  Pallas kernels: 190 us -> 179 us
    pallas_call x1, Pallas kernels: 190 us -> 179 us  [on_device_aligned(): pl.pallas_call(functools.partial(layer_kernel, dp, sizes), out_shape=jax....]
where the time goes in v3:
time: 186 us; the launch traced here: 183 us
  Pallas kernels  179 us (96%)
  local copies, waits for them, and re-layouts  2.7 us (1%)
    pallas_call x1, Pallas kernels, on_device_aligned(): pl.pallas_call(functools.partial(layer_kernel, dp, sizes), out_shape=jax....  179 us

profile of v3, /device:TPU:27, one launch (start us, length us, event | category | flops | bytes accessed | tf_op | source)
XLA Modules:
  0.0 183.2 jit_solution(14247669701412561917)
XLA Ops:
  0.0 0.9 convert_reduce_fusion
  0.9 0.6 select_reduce_fusion.order_ref
  1.5 178.9 %layer.1 = bf16[320,2560]{1,0:T(8,128)(2,1)} custom-call(s32[16]{0:T(128)} %select_reduce_fusion.order_ref, f32[1280]{0:T(1024)} %refs_0_.1, f32[1280]{0:T(1024)} %refs_1_.1, f32[1280]{0:T(1024)} %refs_2_.1, f32[1280]{0:T(1024)} %refs_3_.1, f32[2,512]{1,0:T(2,128)} %refs_4_.1, f32[640]{0:T(1024)} %refs_5_.1, f32[640]{0:T(1024)} %refs_6_.1, f32[2560]{0:T(1024)} %refs_7_.1, ...), custom_call_target="tpu_custom_call" | custom-call | tf_op jit(solution)/shard_map/layer/pallas_call | solution.py:756
  180.5 2.7 %copy.16 = bf16[1,1,320,2560]{3,2,1,0:T(8,128)(2,1)} copy(bf16[1,1,320,2560]{3,2,1,0:T(8,128)(2,1)} %bitcast.3) | data formatting | bytes 3276800

commit v4 on v3

--- a/solution.py
+++ b/solution.py
@@ -177,28 +177,28 @@
 
 
 class Gather:
-    def __init__(self, me, h, dp, parts, send, recv):
-        self.h, self.parts, self.send, self.recv = h, parts, send, recv
+    def __init__(self, me, h, dp, parts, send, recv, near):
+        self.h, self.parts, self.send, self.recv, self.near = h, parts, send, recv, near
         self.sides = 2
         self.length = dp // (self.sides * CORES)
         self.core = lax.rem(me, CORES)
         self.side = lax.rem(lax.div(me, CORES), self.sides)
         self.z = lax.div(me, CORES * self.sides)
-        self.started = []
 
     def index(self, z, side, core):
         return (z * self.sides + side) * CORES + core
 
-    def copy(self, t, origin, route):
+    def copy(self, t, origin, route, count=1):
         target = {
             UP: lambda: self.index(self.z + 1, self.side, self.core),
             DOWN: lambda: self.index(self.z - 1, self.side, self.core),
             SIDE: lambda: self.index(self.z, 1 - self.side, self.core),
             CORE: lambda: self.index(self.z, self.side, 1 - self.core),
         }[route]()
-        ref = self.parts[t](origin)
+        ref = self.parts[t](origin, count)
+        near = self.near.at[t] if route == CORE else self.recv.at[t, lax.div(origin, CORES)]
         return pltpu.make_async_remote_copy(
-            ref, ref, self.send.at[t, route, origin], self.recv.at[t, origin], (target, self.h), MESH
+            ref, ref, self.send.at[t, route], near, (target, self.h), MESH
         )
 
     def go(self, t, origin, routes, act):
@@ -214,26 +214,23 @@
     def own(self, t, act, routes=(UP, DOWN, SIDE, CORE)):
         self.go(t, self.index(self.z, self.side, self.core), routes, act)
 
-    def line(self, t, s, act, arrive=True):
+    def line(self, t, s, act):
         @pl.when(self.z >= s)
         def _():
             origin = self.index(self.z - s, self.side, self.core)
-            if arrive:
-                self.copy(t, origin, CORE).wait_recv()
+            self.copy(t, origin, SIDE).wait_recv()
             self.go(t, origin, (UP, SIDE, CORE), act)
 
         @pl.when(self.z + s < self.length)
         def _():
             origin = self.index(self.z + s, self.side, self.core)
-            if arrive:
-                self.copy(t, origin, CORE).wait_recv()
+            self.copy(t, origin, SIDE).wait_recv()
             self.go(t, origin, (DOWN, SIDE, CORE), act)
 
-    def across(self, t, s, act, arrive=True):
+    def across(self, t, s, act):
         def one(z):
             origin = self.index(z, 1 - self.side, self.core)
-            if arrive:
-                self.copy(t, origin, CORE).wait_recv()
+            self.copy(t, origin, SIDE).wait_recv()
             self.go(t, origin, (CORE,), act)
 
         if s == 0:
@@ -242,42 +239,33 @@
         pl.when(self.z >= s)(lambda: one(self.z - s))
         pl.when(self.z + s < self.length)(lambda: one(self.z + s))
 
-    def twin(self, t, act, arrive=True):
+    def twin(self, t, act):
         origin = self.index(self.z, 1 - self.side, self.core)
-        if arrive:
-            self.copy(t, origin, CORE).wait_recv()
+        self.copy(t, origin, SIDE).wait_recv()
         self.go(t, origin, (UP, DOWN, CORE), act)
 
-    def both(self, t, s, act, arrive=True):
+    def both(self, t, s, act):
         def one(z, route):
             for side in range(self.sides):
                 origin = self.index(z, side, self.core)
-                if arrive:
-                    self.copy(t, origin, CORE).wait_recv()
+                self.copy(t, origin, SIDE).wait_recv()
                 self.go(t, origin, (route, CORE), act)
 
         pl.when(self.z >= s)(lambda: one(self.z - s, UP))
         pl.when(self.z + s < self.length)(lambda: one(self.z + s, DOWN))
 
     def rest(self, t):
-        def one(k):
-            origin = k * CORES + 1 - self.core
-            self.copy(t, origin, CORE).wait_recv()
-
-        loop(0, self.length * self.sides, one)
+        self.copy(t, 0, CORE, self.length * self.sides).wait_recv()
 
     def finish(self, t, paired):
-        act = lambda copy: copy.wait_send()
-        self.own(t, act)
-        if paired:
-            self.twin(t, act, False)
-            for s in range(1, self.length):
-                self.both(t, s, act, False)
-            return
-        for s in range(1, self.length):
-            self.line(t, s, act, False)
-        for s in range(self.length):
-            self.across(t, s, act, False)
+        each = self.sides if paired else 1
+        self.copy(t, 0, CORE, self.length * self.sides).wait_send()
+        self.copy(t, 0, SIDE, 1 if paired else self.length).wait_send()
+        for z in range(self.length - 1):
+            up = self.copy(t, 0, UP, (z + 1) * each)
+            pl.when(self.z == z)(lambda copy=up: copy.wait_send())
+            down = self.copy(t, 0, DOWN, (z + 1) * each)
+            pl.when(self.z == self.length - 1 - z)(lambda copy=down: copy.wait_send())
 
 
 def layer_kernel(
@@ -340,6 +328,7 @@
     placed,
     wsend,
     wrecv,
+    wnear,
     own_sem,
     xs,
     xr,
@@ -350,8 +339,10 @@
     cr,
     s1,
     r1,
+    l1,
     s2,
     r2,
+    l2,
     s3,
     r3,
     fs,
@@ -384,15 +375,18 @@
     loop(1, dp, hello)
     pl.semaphore_signal(barrier, inc=1, device_id=peer, device_id_type=MESH)
 
+    def span(d, rows, count):
+        return pl.ds(pl.multiple_of(d * rows, rows), rows * count)
+
     parts = [
-        lambda d: all_q.at[:, at_rows(d, wq_ref.shape[1]), :],
-        lambda d: all_o.at[:, at_rows(d, wo_ref.shape[0]), :],
-        lambda d: all_1.at[at_rows(d, w1_ref.shape[0]), : units // 2],
-        lambda d: all_1.at[at_rows(d, w1_ref.shape[0]), units // 2 :],
-        lambda d: all_2.at[at_rows(d, w2_ref.shape[0]), at_rows(there, width)],
-        lambda d: all_2.at[at_rows(d, w2_ref.shape[0]), at_rows(h, width)],
+        lambda d, n=1: all_q.at[:, span(d, wq_ref.shape[1], n), :],
+        lambda d, n=1: all_o.at[:, span(d, wo_ref.shape[0], n), :],
+        lambda d, n=1: all_1.at[span(d, w1_ref.shape[0], n), : units // 2],
+        lambda d, n=1: all_1.at[span(d, w1_ref.shape[0], n), units // 2 :],
+        lambda d, n=1: all_2.at[span(d, w2_ref.shape[0], n), at_rows(there, width)],
+        lambda d, n=1: all_2.at[span(d, w2_ref.shape[0], n), at_rows(h, width)],
     ]
-    net = Gather(me, h, dp, parts, wsend, wrecv)
+    net = Gather(me, h, dp, parts, wsend, wrecv, wnear)
     mine = [
         pltpu.make_async_copy(wq_ref, parts[0](me), own_sem.at[0]),
         pltpu.make_async_copy(
@@ -503,10 +497,14 @@
 
     def ctx_copy(b, p):
         ref = ctx.at[at_rows(b, block), at_rows(h * pairs + p, PAIR)]
-        return pltpu.make_async_remote_copy(ref, ref, cs.at[b, p], cr.at[b, p], peer, MESH)
+        return pltpu.make_async_remote_copy(ref, ref, cs.at[b], cr.at[b], peer, MESH)
+
+    def ctx_all(b):
+        ref = ctx.at[at_rows(b, block), at_rows(h, columns)]
+        return pltpu.make_async_remote_copy(ref, ref, cs.at[b], cr.at[b], peer, MESH)
 
     def attended(b):
-        loop(0, pairs, lambda p: ctx_copy(b, p).wait_recv())
+        ctx_all(b).wait_recv()
         at = at_rows(b, block)
         total = x[at, at_rows(h, width)].astype(jnp.float32) + par(ob, width)
         for i in range(2):
@@ -526,20 +524,28 @@
     def one(b, n):
         other = lax.rem(me + n, dp)
         return pltpu.make_async_remote_copy(
-            piece(att, b, other), home(b, me), s1.at[b, n], r1.at[b, n], (other, h), MESH
+            piece(att, b, other), home(b, me), s1.at[b], r1.at[b], (other, h), MESH
         )
 
+    def one_all(b):
+        ref = att.at[: (dp - 1) * rows]
+        return pltpu.make_async_remote_copy(ref, ref, s1.at[b], r1.at[b], peer, MESH)
+
     def one_own(b):
-        return pltpu.make_async_copy(piece(att, b, me), home(b, me), r1.at[b, 0])
+        return pltpu.make_async_copy(piece(att, b, me), home(b, me), l1.at[b])
 
     def two(b, n):
         other = lax.rem(me + n, dp)
         return pltpu.make_async_remote_copy(
-            second.at[b, other], piece(placed, b, me), s2.at[b, n], r2.at[b, n], (other, h), MESH
+            second.at[b, other], piece(placed, b, me), s2.at[b], r2.at[b], (other, h), MESH
         )
 
+    def two_all(b):
+        ref = placed.at[: (dp - 1) * rows]
+        return pltpu.make_async_remote_copy(ref, ref, s2.at[b], r2.at[b], peer, MESH)
+
     def two_own(b):
-        return pltpu.make_async_copy(second.at[b, me], piece(placed, b, me), r2.at[b, 0])
+        return pltpu.make_async_copy(second.at[b, me], piece(placed, b, me), l2.at[b])
 
     def three(b):
         ref = full.at[at_rows(b, block), at_rows(h, width)]
@@ -551,7 +557,7 @@
 
     def arrive(b):
         one_own(b).wait()
-        loop(1, dp, lambda n: one(b, n).wait_recv())
+        one_all(b).wait_recv()
         three(b).start()
 
     def share(b, target):
@@ -607,7 +613,7 @@
 
     def store(b):
         two_own(b).wait()
-        loop(1, dp, lambda n: two(b, n).wait_recv())
+        two_all(b).wait_recv()
         loop(0, block // chunk, lambda i: done_copy(b, i).start())
 
     def when(i, offset, body):
@@ -633,8 +639,8 @@
             x_copy(j).wait_send()
 
         def block_sent(b):
-            loop(0, pairs, lambda p: ctx_copy(b, p).wait_send())
-            loop(1, dp, lambda n: one(b, n).wait_send())
+            ctx_all(b).wait_send()
+            one_all(b).wait_send()
 
         loop(0, blocks, block_sent)
         for t in range(5):
@@ -684,7 +690,7 @@
     def last(b):
         three(b).wait_send()
         out_copy(b).wait_send()
-        loop(1, dp, lambda n: two(b, n).wait_send())
+        two_all(b).wait_send()
         loop(0, block // chunk, lambda i: done_copy(b, i).wait())
 
     loop(0, blocks, last)
@@ -696,12 +702,12 @@
         U(3), L(0, 3), S(4), U(4), A(0, 2), L(2, 1), A(0, 3),
     ]
     during = {
-        0: [L(3, 1)], 1: [B(1, 3)], 2: [L(4, 1)], 6: [L(2, 2)], 10: [L(3, 2)], 14: [L(4, 2)],
-        18: [L(2, 3)],
+        0: [L(3, 1)], 1: [B(1, 3)], 2: [L(4, 1)], 6: [L(2, 2)], 10: [L(3, 2)], 13: [L(4, 2)],
+        16: [L(2, 3)], 19: [L(3, 3)],
     }
     after = {
-        4: [S(5), U(5)], 5: [L(3, 3), A(2, 0), A(3, 0), A(4, 0), A(2, 1), A(3, 1), A(4, 1)],
-        6: [L(4, 3), L(5, 1), A(2, 2), A(3, 2), A(4, 2), A(2, 3), A(3, 3)], 7: [L(5, 2), A(4, 3)],
+        4: [S(5), U(5)], 5: [L(4, 3), A(2, 0), A(3, 0), A(4, 0), A(2, 1), A(3, 1), A(4, 1)],
+        6: [L(5, 1), A(2, 2), A(3, 2), A(4, 2), A(2, 3), A(3, 3)], 7: [L(5, 2), A(4, 3)],
         8: [L(5, 3), A(5, 0)], 9: [A(5, 1)], 10: [A(5, 2)], 11: [A(5, 3)],
     }
     return before, during, after
@@ -749,7 +755,7 @@
         "offsets": offsets,
         "lengths": [value.shape[-1] for value in values],
         "plan": plan,
-        "stages": (2, 7, 12, 14),
+        "stages": (3, 7, 12, 14),
     }
     bf16, f32 = jnp.bfloat16, jnp.float32
     dma = pltpu.SemaphoreType.DMA
@@ -780,20 +786,23 @@
             pltpu.VMEM((blocks, block, width), bf16),
             pltpu.VMEM((dp, rows, width), bf16),
             pltpu.VMEM((frames, width), bf16),
-            dma((6, 4, dp)),
-            dma((6, dp)),
+            dma((6, 4)),
+            dma((6, dp // CORES)),
+            dma((6,)),
             dma((4,)),
             dma((4,)),
             dma((4,)),
             dma((4,)),
             dma,
             dma,
-            dma((blocks, columns // PAIR)),
-            dma((blocks, columns // PAIR)),
-            dma((blocks, dp)),
-            dma((blocks, dp)),
-            dma((blocks, dp)),
-            dma((blocks, dp)),
+            dma((blocks,)),
+            dma((blocks,)),
+            dma((blocks,)),
+            dma((blocks,)),
+            dma((blocks,)),
+            dma((blocks,)),
+            dma((blocks,)),
+            dma((blocks,)),
             dma((blocks,)),
             dma((blocks,)),
             dma((blocks,)),

time: 186 us -> 172 us (0.925); the launches traced: 183 us -> 172 us
  Pallas kernels: 179 us -> 167 us
    pallas_call x1, Pallas kernels: 179 us -> 167 us  [on_device_aligned(): pl.pallas_call(functools.partial(layer_kernel, dp, sizes), out_shape=jax....]
where the time goes in v4:
time: 172 us
  Pallas kernels  167 us (97%)
  local copies, waits for them, and re-layouts  2.7 us (2%)
    pallas_call x1, Pallas kernels, on_device_aligned(): pl.pallas_call(functools.partial(layer_kernel, dp, sizes), out_shape=jax....  167 us

profile of v4, /device:TPU:27, one launch (start us, length us, event | category | flops | bytes accessed | tf_op | source)
XLA Modules:
  0.0 171.6 jit_solution(1678949830851208769)
XLA Ops:
  0.0 0.9 convert_reduce_fusion
  0.9 0.6 select_reduce_fusion.order_ref
  1.5 167.3 %layer.1 = bf16[320,2560]{1,0:T(8,128)(2,1)} custom-call(s32[16]{0:T(128)} %select_reduce_fusion.order_ref, f32[1280]{0:T(1024)} %refs_0_.1, f32[1280]{0:T(1024)} %refs_1_.1, f32[1280]{0:T(1024)} %refs_2_.1, f32[1280]{0:T(1024)} %refs_3_.1, f32[2,512]{1,0:T(2,128)} %refs_4_.1, f32[640]{0:T(1024)} %refs_5_.1, f32[640]{0:T(1024)} %refs_6_.1, f32[2560]{0:T(1024)} %refs_7_.1, ...), custom_call_target="tpu_custom_call" | custom-call | tf_op jit(solution)/shard_map/layer/pallas_call | solution.py:762
  168.9 2.7 %copy.16 = bf16[1,1,320,2560]{3,2,1,0:T(8,128)(2,1)} copy(bf16[1,1,320,2560]{3,2,1,0:T(8,128)(2,1)} %bitcast.3) | data formatting | bytes 3276800

commit v5 on v4

--- a/solution.py
+++ b/solution.py
@@ -699,7 +699,7 @@
 def plan(L, A, B, S, U, out_own, out_twin):
     before = [
         out_own, S(2), L(0, 1), out_twin, B(1, 1), U(2), L(0, 2), S(3), A(0, 0), A(0, 1), B(1, 2),
-        U(3), L(0, 3), S(4), U(4), A(0, 2), L(2, 1), A(0, 3),
+        L(0, 3), U(3), S(4), U(4), A(0, 2), L(2, 1), A(0, 3),
     ]
     during = {
         0: [L(3, 1)], 1: [B(1, 3)], 2: [L(4, 1)], 6: [L(2, 2)], 10: [L(3, 2)], 13: [L(4, 2)],

time: 172 us -> 172 us (level)
  no operation moved by 1% of the time
where the time goes in v5:
time: 172 us
  Pallas kernels  167 us (97%)
  local copies, waits for them, and re-layouts  2.7 us (2%)
    pallas_call x1, Pallas kernels, on_device_aligned(): pl.pallas_call(functools.partial(layer_kernel, dp, sizes), out_shape=jax....  167 us

profile of v5, /device:TPU:27, one launch (start us, length us, event | category | flops | bytes accessed | tf_op | source)
XLA Modules:
  0.0 171.6 jit_solution(4708710115514460188)
XLA Ops:
  0.0 0.9 convert_reduce_fusion
  0.9 0.6 select_reduce_fusion.order_ref
  1.5 167.3 %layer.1 = bf16[320,2560]{1,0:T(8,128)(2,1)} custom-call(s32[16]{0:T(128)} %select_reduce_fusion.order_ref, f32[1280]{0:T(1024)} %refs_0_.1, f32[1280]{0:T(1024)} %refs_1_.1, f32[1280]{0:T(1024)} %refs_2_.1, f32[1280]{0:T(1024)} %refs_3_.1, f32[2,512]{1,0:T(2,128)} %refs_4_.1, f32[640]{0:T(1024)} %refs_5_.1, f32[640]{0:T(1024)} %refs_6_.1, f32[2560]{0:T(1024)} %refs_7_.1, ...), custom_call_target="tpu_custom_call" | custom-call | tf_op jit(solution)/shard_map/layer/pallas_call | solution.py:762
  168.9 2.7 %copy.16 = bf16[1,1,320,2560]{3,2,1,0:T(8,128)(2,1)} copy(bf16[1,1,320,2560]{3,2,1,0:T(8,128)(2,1)} %bitcast.3) | data formatting | bytes 3276800
